TPU v7x, 128 devices: a whole 4x4x4 slice. The times are simulated.
128 devices in a mesh: box: 8 (over z, y_lo), dir: 16 (over y_hi, x, core).
Axes of the slice: x: 4, y: 4 (y_hi: 2, y_lo: 2; y = y_hi * 2 + y_lo), z: 4, core: 2. Of those that a mesh axis runs over, the one named last changes fastest.
Arguments:
- leaf_out: bfloat16 [2, 8192, 1024], P(None, ('box', 'dir')), may hold values from -6 to 6
- interp_mid: bfloat16 [1024, 4096], replicated, may hold values from -0.1875 to 0.1875
- shift_mid: float32 [8, 4096], replicated, may hold values from -3.140625 to 3.140625
- trans_mid: float32 [2, 316, 4096], P(None, None, 'dir'), may hold values from -0.5 to 0.5
- list_mid: int32 [1024, 64], replicated, may hold values from 0 to 1023
- offset_mid: int32 [1024, 64], replicated, may hold values from 0 to 315
- interp_top: bfloat16 [16, 256, 1024], P('dir'), may hold values from -0.375 to 0.375
- shift_top: float32 [8, 16, 1024], P(None, 'dir'), may hold values from -3.140625 to 3.140625
- trans_top: float32 [2, 316, 16, 1024], P(None, None, 'dir', 'box'), may hold values from -0.5 to 0.5
- list_top: int32 [128, 64], replicated, may hold values from 0 to 127
- offset_top: int32 [128, 64], replicated, may hold values from 0 to 315
Outputs:
- leaf_in: float32 [2, 8192, 1024], P(None, ('box', 'dir'))
Inputs may be any that keep to these rules, and one draw needn't show every extreme that they name: `list_mid`: middle box indices. `offset_mid`: offset indices. `list_top`: top box indices. `offset_top`: offset indices.
All inputs are finite; a program needn't handle non-finite values.
Results may differ from a plain program's by a relative error of at most 0.014.
Values may be sent and summed in bfloat16 or wider, within the bound.
A program may use at most 64 MiB of HBM per device.

v0:
```python
import math

import jax
import jax.numpy as jnp
from jax import lax
from jax.sharding import PartitionSpec as P


def from_everyone(value, axis):
    copies = jnp.broadcast_to(value, (lax.axis_size(axis), *value.shape))
    return lax.all_to_all(copies, axis, split_axis=0, concat_axis=0, tiled=True)


def joined_along(pieces, dim):
    lengths = list(pieces.shape[1:])
    lengths[dim] *= pieces.shape[0]
    return jnp.moveaxis(pieces, 0, dim).reshape(lengths)


def gather_directly(value, axis, dim):
    pieces = from_everyone(value, axis)
    return joined_along(pieces, dim)


def in_blocks(value, dim, count):
    before, after = (value.shape[:dim], value.shape[dim + 1 :])
    return jnp.moveaxis(value.reshape(*before, count, -1, *after), dim, 0)


def sum_at_owner(value, axis, dim):
    count = lax.axis_size(axis)
    pieces = lax.all_to_all(in_blocks(value, dim, count), axis, 0, 0, tiled=True)
    return jnp.sum(pieces.astype(jnp.float32), axis=0)


def complex_translate(patterns, sources, offsets, operators):
    row_count = sources.shape[0]
    list_width = sources.shape[1]
    block_rows = math.gcd(row_count, 32)
    source_count = patterns.shape[1]
    offset_count = operators.shape[1]
    width = patterns.shape[2]
    source_blocks = sources.reshape(row_count // block_rows, block_rows * list_width)
    offset_blocks = offsets.reshape(row_count // block_rows, block_rows * list_width)

    def one_block(indices):
        source_hot = (indices[0][:, None] == lax.iota(jnp.int32, source_count)[None, :]).astype(
            jnp.bfloat16
        )
        offset_hot = (indices[1][:, None] == lax.iota(jnp.int32, offset_count)[None, :]).astype(
            jnp.float32
        )
        picked = jnp.einsum("rn,cnk->crk", source_hot, patterns, preferred_element_type=jnp.float32)
        factors = jnp.einsum("ro,cok->crk", offset_hot, operators)
        picked = picked.reshape(2, block_rows, list_width, width)
        factors = factors.reshape(2, block_rows, list_width, width)
        real_part = jnp.sum(picked[0] * factors[0] - picked[1] * factors[1], axis=1)
        imag_part = jnp.sum(picked[0] * factors[1] + picked[1] * factors[0], axis=1)
        return jnp.stack([real_part, imag_part])

    blocks = lax.map(one_block, (source_blocks, offset_blocks))
    return jnp.transpose(blocks, (1, 0, 2, 3)).reshape(2, row_count, width)


def interpolate_shift(leaves_part, matrix, cos_table, sin_table):
    row_count = leaves_part.shape[1]
    real_part = jnp.dot(leaves_part[0], matrix, preferred_element_type=jnp.float32)
    imag_part = jnp.dot(leaves_part[1], matrix, preferred_element_type=jnp.float32)
    octant = lax.iota(jnp.int32, row_count) % 8
    selector = (octant[:, None] == lax.iota(jnp.int32, 8)[None, :]).astype(jnp.float32)
    cos_rows = jnp.dot(selector, cos_table)
    sin_rows = jnp.dot(selector, sin_table)
    return jnp.stack(
        [real_part * cos_rows - imag_part * sin_rows, real_part * sin_rows + imag_part * cos_rows]
    )


def sum_children(values):
    return jnp.sum(values.reshape(2, values.shape[1] // 8, 8, values.shape[2]), axis=2)


def child_shift(parents, cos_table, sin_table):
    real_part = parents[0].astype(jnp.float32)[:, None, :]
    imag_part = parents[1].astype(jnp.float32)[:, None, :]
    new_real = real_part * cos_table[None] + imag_part * sin_table[None]
    new_imag = imag_part * cos_table[None] - real_part * sin_table[None]
    return jnp.stack([new_real, new_imag]).reshape(2, -1, cos_table.shape[1]).astype(jnp.bfloat16)


def adjoint_apply(children, matrix):
    dims = (((1,), (1,)), ((), ()))
    real_part = lax.dot_general(children[0], matrix, dims, preferred_element_type=jnp.float32)
    imag_part = lax.dot_general(children[1], matrix, dims, preferred_element_type=jnp.float32)
    return jnp.stack([real_part, imag_part])


def on_device(
    leaf_out,
    interp_mid,
    shift_mid,
    trans_mid,
    list_mid,
    offset_mid,
    interp_top,
    shift_top,
    trans_top,
    list_top,
    offset_top,
):
    box_index = lax.axis_index("box")
    sector = trans_mid.shape[2]
    top_width = trans_top.shape[3]
    cos_mid = jnp.cos(shift_mid)
    sin_mid = jnp.sin(shift_mid)
    shifted = interpolate_shift(leaf_out, interp_mid, cos_mid, sin_mid)
    own_parents = sum_children(shifted).astype(jnp.bfloat16)
    mid_pattern = lax.all_to_all(own_parents, "dir", split_axis=2, concat_axis=1, tiled=True)
    mid_group = mid_pattern.shape[1]
    mid_all = gather_directly(mid_pattern, "box", 1)
    own_list = lax.dynamic_slice_in_dim(list_mid, box_index * mid_group, mid_group, 0)
    own_offsets = lax.dynamic_slice_in_dim(offset_mid, box_index * mid_group, mid_group, 0)
    mid_far = complex_translate(mid_all, own_list, own_offsets, trans_mid)
    table_top = interp_top[0]
    cos_top = jnp.cos(shift_top[:, 0, :])
    sin_top = jnp.sin(shift_top[:, 0, :])
    scale_top = sector / table_top.shape[1]
    columns_top = lax.dynamic_slice_in_dim(table_top, box_index * top_width, top_width, 1)
    cos_owned = lax.dynamic_slice_in_dim(cos_top, box_index * top_width, top_width, 1)
    sin_owned = lax.dynamic_slice_in_dim(sin_top, box_index * top_width, top_width, 1)
    top_pattern = sum_children(
        interpolate_shift(mid_all, columns_top, cos_owned, sin_owned)
    ).astype(jnp.bfloat16)
    top_in = complex_translate(top_pattern, list_top, offset_top, trans_top[:, :, 0, :]).astype(
        jnp.bfloat16
    )
    children = child_shift(top_in, cos_owned, sin_owned)
    partial_terms = adjoint_apply(children, columns_top)
    down_top = sum_at_owner(partial_terms.astype(jnp.bfloat16), "box", 1)
    mid_in = (mid_far + scale_top * down_top).astype(jnp.bfloat16)
    parents = lax.all_to_all(mid_in, "dir", split_axis=1, concat_axis=2, tiled=True)
    leaf_children = child_shift(parents, cos_mid, sin_mid)
    scale_leaf = interp_mid.shape[0] / interp_mid.shape[1]
    return scale_leaf * adjoint_apply(leaf_children, interp_mid)


def solution(mesh):
    return jax.shard_map(
        on_device,
        mesh=mesh,
        in_specs=(
            P(None, ("box", "dir"), None),
            P(),
            P(),
            P(None, None, "dir"),
            P(),
            P(),
            P("dir", None, None),
            P(None, "dir", None),
            P(None, None, "dir", "box"),
            P(),
            P(),
        ),
        out_specs=P(None, ("box", "dir"), None),
        check_vma=False,
    )
```

profile of v0, /device:TPU:1, one launch (start us, length us, event | category | flops | bytes accessed | tf_op | source)
XLA Modules:
  0.0 143.7 jit_solution(15926381439773424269)
XLA Ops:
  0.0 5.2 %fusion.37 = f32[64,4096]{1,0:T(8,128)S(1)} fusion(bf16[1024,4096]{1,0:T(8,128)(2,1)} %param.16, bf16[2,64,1024]{2,1,0:T(8,128)(2,1)} %param.15), kind=kOutput, calls=%fused_computation.66 | convolution fusion | flops 536870912 | bytes 9568256 | tf_op jit(solution)/shard_map/dot_general | solution.py:68
  5.2 0.7 copy-done.1
  5.9 1.6 %fusion.39 = f32[64,4096]{1,0:T(8,128)S(1)} fusion(bf16[1024,4096]{1,0:T(8,128)(2,1)S(1)} %copy-done.1, bf16[2,64,1024]{2,1,0:T(8,128)(2,1)S(1)} %copy-done.2), kind=kOutput, calls=%fused_computation.68 | convolution fusion | flops 536870912 | bytes 9568256 | tf_op jit(solution)/shard_map/dot_general | solution.py:67
  7.5 0.5 fusion.65
  8.0 0.3 fusion.53
  8.3 0.5 subtract_bitcast_fusion
  8.8 0.5 maximum_reduce_fusion
  9.3 2.8 %copy.54 = bf16[2,8,4096]{1,0,2:T(2,128)(2,1)S(1)} copy(bf16[2,8,4096]{2,1,0:T(8,128)(2,1)S(1)} %maximum_reduce_fusion) | data formatting | bytes 262144 | tf_op jit(solution)/shard_map/convert_element_type | solution.py:116
  12.1 2.2 %reshape.383 = bf16[16,2,2048]{2,1,0:T(2,128)(2,1)S(1)} reshape(bf16[4096,2,8]{2,1,0:T(2,128)(2,1)S(1)} %bitcast.204) | data formatting | bytes 262144
  14.3 15.8 %all_to_all.43 = bf16[16,2,2048]{2,1,0:T(2,128)(2,1)S(1)} all-to-all(bf16[16,2,2048]{2,1,0:T(2,128)(2,1)S(1)} %reshape.383), channel_id=1, replica_groups=mesh['box'=8,'dir'=16] {'dir'}, dimensions={0} | all-to-all | bytes 262144 | tf_op jit(solution)/shard_map/all_to_all | solution.py:117
  30.1 2.4 %reshape.384 = bf16[4096,2,8]{2,1,0:T(2,128)(2,1)S(1)} reshape(bf16[16,2,2048]{2,1,0:T(2,128)(2,1)S(1)} %all_to_all.43) | data formatting | bytes 262144
  32.5 1.2 copy.67
  33.8 1.1 broadcast_in_dim.18
  34.9 5.3 %all-to-all-start.1 = ((bf16[8,2,128,256]{3,2,1,0:T(8,128)(2,1)}), bf16[8,2,128,256]{3,2,1,0:T(8,128)(2,1)S(1)}, u32[]{:S(2)}, u32[]{:S(2)}) async-start(bf16[8,2,128,256]{3,2,1,0:T(8,128)(2,1)} %broadcast_in_dim.18), calls=%async_computation.1 | async-start | bytes 2097152 | tf_op jit(solution)/shard_map/all_to_all | solution.py:11
  40.2 0.8 constant_dynamic-slice_fusion.4
  41.0 0.7 reshape.366
  41.9 0.7 reshape.368
  43.1 0.8 dynamic-slice_cosine_fusion
  44.2 11.0 %all-to-all-done.1 = bf16[8,2,128,256]{3,2,1,0:T(8,128)(2,1)S(1)} async-done(((bf16[8,2,128,256]{3,2,1,0:T(8,128)(2,1)}), bf16[8,2,128,256]{3,2,1,0:T(8,128)(2,1)S(1)}, u32[]{:S(2)}, u32[]{:S(2)}) %all-to-all-start.1) | async-done | bytes 1048608 | tf_op jit(solution)/shard_map/all_to_all | solution.py:11
  55.2 1.1 copy.82
  56.2 1.3 fusion.64
  58.1 0.8 subtract_bitcast_fusion.1
  59.2 11.3 %while.21 = (s32[]{:T(128)}, bf16[4,2,32,128]{3,2,1,0:T(8,128)(2,1)}, s32[4,2048]{1,0:T(4,128)S(1)}, bf16[2,128,128]{2,1,0:T(8,128)(2,1)S(1)}, s32[4,2048]{1,0:T...) while((s32[]{:T(128)}, bf16[4,2,32,128]{3,2,1,0:T(8,128)(2,1)}, ...), condition=%wide.region_9.10_spmd, body=%wide.region_6.9_spmd.sunk | while | flops 468598784 | bytes 12908653 | solution.py:61
  59.2 1.0 convolution_bitcast_fusion.9
  60.3 0.7 convolution_bitcast_fusion.10
  61.4 0.6 fusion.104
  62.0 1.0 convolution_bitcast_fusion.9
  63.1 0.7 convolution_bitcast_fusion.10
  64.2 0.6 fusion.104
  64.9 1.0 convolution_bitcast_fusion.9
  65.9 0.7 convolution_bitcast_fusion.10
  67.1 0.6 fusion.104
  67.7 1.0 convolution_bitcast_fusion.9
  68.7 0.7 convolution_bitcast_fusion.10
  69.9 0.6 fusion.104
  70.5 0.8 fusion.66
  72.2 1.0 copy.63
  73.2 4.4 %all-to-all-start.2 = ((bf16[8,2,128,256]{3,2,1,0:T(8,128)(2,1)}), bf16[8,2,128,256]{3,2,1,0:T(8,128)(2,1)}, u32[]{:S(2)}, u32[]{:S(2)}) async-start(bf16[8,2,128,256]{3,2,1,0:T(8,128)(2,1)} %copy.63), calls=%async_computation.2 | async-start | bytes 2097152 | tf_op jit(solution)/shard_map/all_to_all | solution.py:32
  77.7 38.9 %while.20 = (s32[]{:T(128)}, f32[4,2,32,256]{3,2,0,1:T(8,128)S(1)}, s32[4,2048]{1,0:T(4,128)}, bf16[2,1024,256]{2,1,0:T(8,128)(2,1)}, s32[4,2048]{1,0:T(4,128)},...) while((s32[]{:T(128)}, f32[4,2,32,256]{3,2,0,1:T(8,128)S(1)}, s32[4,2048]{1,0:T(4,128)}, ...), condition=%wide.region_4.5_spmd, body=%wide.region_1.4_spmd.sunk | while | flops 2817122304 | bytes 26783852 | solution.py:61
  77.7 0.8 constant_dynamic-slice_fusion.8
  78.5 1.3 convolution_bitcast_fusion.8
  79.8 3.6 %fusion.98 = f32[2,2048,256]{2,1,0:T(8,128)S(1)} fusion(bf16[2,1024,256]{2,1,0:T(8,128)(2,1)} %get-tuple-element.270, s32[2048]{0:T(1024)S(1)} %bitcast.225), kind=kOutput, calls=%fused_computation.4.clone.1 | convolution fusion | flops 2149580800 | bytes 5251072 | tf_op jit(solution)/shard_map/while/body/eval_jaxpr/rn,cnk->crk/dot_general | solution.py:53
  83.4 1.9 %multiply_subtract_fusion.4 = (f32[1,2048,256]{2,1,0:T(8,128)S(1)}, f32[1,2048,256]{2,1,0:T(8,128)}) fusion(f32[2,2048,256]{2,1,0:T(8,128)S(1)} %convolution_bitcast_fusion.8, f32[2,2048,256]{2,1,0:T(8,128)S(1)} %fusion.98), kind=kLoop, calls=%fused_computation.9.clone.1 | loop fusion | flops 3145728 | bytes 12582912 | tf_op jit(solution)/shard_map/while/body/eval_jaxpr/sub | solution.py:57
  85.3 1.8 %reduce_sum.73 = f32[32,256]{1,0:T(8,128)S(1)} reduce(f32[32,64,256]{2,1,0:T(8,128)} %bitcast.201, f32[]{:T(128)} %constant.54.clone.1..sunk), dimensions={1}, to_apply=%region_3.3 | reduce | flops 516096 | bytes 2129924 | tf_op jit(solution)/shard_map/while/body/eval_jaxpr/reduce_sum | solution.py:58
  87.4 0.8 constant_dynamic-slice_fusion.8
  88.2 1.3 convolution_bitcast_fusion.8
  89.5 3.6 %fusion.98 = f32[2,2048,256]{2,1,0:T(8,128)S(1)} fusion(bf16[2,1024,256]{2,1,0:T(8,128)(2,1)} %get-tuple-element.270, s32[2048]{0:T(1024)S(1)} %bitcast.225), kind=kOutput, calls=%fused_computation.4.clone.1 | convolution fusion | flops 2149580800 | bytes 5251072 | tf_op jit(solution)/shard_map/while/body/eval_jaxpr/rn,cnk->crk/dot_general | solution.py:53
  93.2 1.9 %multiply_subtract_fusion.4 = (f32[1,2048,256]{2,1,0:T(8,128)S(1)}, f32[1,2048,256]{2,1,0:T(8,128)}) fusion(f32[2,2048,256]{2,1,0:T(8,128)S(1)} %convolution_bitcast_fusion.8, f32[2,2048,256]{2,1,0:T(8,128)S(1)} %fusion.98), kind=kLoop, calls=%fused_computation.9.clone.1 | loop fusion | flops 3145728 | bytes 12582912 | tf_op jit(solution)/shard_map/while/body/eval_jaxpr/sub | solution.py:57
  95.0 1.8 %reduce_sum.73 = f32[32,256]{1,0:T(8,128)S(1)} reduce(f32[32,64,256]{2,1,0:T(8,128)} %bitcast.201, f32[]{:T(128)} %constant.54.clone.1..sunk), dimensions={1}, to_apply=%region_3.3 | reduce | flops 516096 | bytes 2129924 | tf_op jit(solution)/shard_map/while/body/eval_jaxpr/reduce_sum | solution.py:58
  97.1 0.8 constant_dynamic-slice_fusion.8
  97.9 1.3 convolution_bitcast_fusion.8
  99.3 3.6 %fusion.98 = f32[2,2048,256]{2,1,0:T(8,128)S(1)} fusion(bf16[2,1024,256]{2,1,0:T(8,128)(2,1)} %get-tuple-element.270, s32[2048]{0:T(1024)S(1)} %bitcast.225), kind=kOutput, calls=%fused_computation.4.clone.1 | convolution fusion | flops 2149580800 | bytes 5251072 | tf_op jit(solution)/shard_map/while/body/eval_jaxpr/rn,cnk->crk/dot_general | solution.py:53
  102.9 1.9 %multiply_subtract_fusion.4 = (f32[1,2048,256]{2,1,0:T(8,128)S(1)}, f32[1,2048,256]{2,1,0:T(8,128)}) fusion(f32[2,2048,256]{2,1,0:T(8,128)S(1)} %convolution_bitcast_fusion.8, f32[2,2048,256]{2,1,0:T(8,128)S(1)} %fusion.98), kind=kLoop, calls=%fused_computation.9.clone.1 | loop fusion | flops 3145728 | bytes 12582912 | tf_op jit(solution)/shard_map/while/body/eval_jaxpr/sub | solution.py:57
  104.8 1.8 %reduce_sum.73 = f32[32,256]{1,0:T(8,128)S(1)} reduce(f32[32,64,256]{2,1,0:T(8,128)} %bitcast.201, f32[]{:T(128)} %constant.54.clone.1..sunk), dimensions={1}, to_apply=%region_3.3 | reduce | flops 516096 | bytes 2129924 | tf_op jit(solution)/shard_map/while/body/eval_jaxpr/reduce_sum | solution.py:58
  106.9 0.8 constant_dynamic-slice_fusion.8
  107.7 1.3 convolution_bitcast_fusion.8
  109.0 3.6 %fusion.98 = f32[2,2048,256]{2,1,0:T(8,128)S(1)} fusion(bf16[2,1024,256]{2,1,0:T(8,128)(2,1)} %get-tuple-element.270, s32[2048]{0:T(1024)S(1)} %bitcast.225), kind=kOutput, calls=%fused_computation.4.clone.1 | convolution fusion | flops 2149580800 | bytes 5251072 | tf_op jit(solution)/shard_map/while/body/eval_jaxpr/rn,cnk->crk/dot_general | solution.py:53
  112.6 1.9 %multiply_subtract_fusion.4 = (f32[1,2048,256]{2,1,0:T(8,128)S(1)}, f32[1,2048,256]{2,1,0:T(8,128)}) fusion(f32[2,2048,256]{2,1,0:T(8,128)S(1)} %convolution_bitcast_fusion.8, f32[2,2048,256]{2,1,0:T(8,128)S(1)} %fusion.98), kind=kLoop, calls=%fused_computation.9.clone.1 | loop fusion | flops 3145728 | bytes 12582912 | tf_op jit(solution)/shard_map/while/body/eval_jaxpr/sub | solution.py:57
  114.5 1.8 %reduce_sum.73 = f32[32,256]{1,0:T(8,128)S(1)} reduce(f32[32,64,256]{2,1,0:T(8,128)} %bitcast.201, f32[]{:T(128)} %constant.54.clone.1..sunk), dimensions={1}, to_apply=%region_3.3 | reduce | flops 516096 | bytes 2129924 | tf_op jit(solution)/shard_map/while/body/eval_jaxpr/reduce_sum | solution.py:58
  116.6 1.4 convert_reduce_fusion
  118.2 12.3 %all_to_all.44 = bf16[2,128,256]{2,0,1:T(2,128)(2,1)S(1)} all-to-all(bf16[2,128,256]{2,0,1:T(2,128)(2,1)S(1)} %copy.64), channel_id=1, replica_groups=mesh['box'=8,'dir'=16] {'dir'}, dimensions={1} | all-to-all | bytes 262144 | tf_op jit(solution)/shard_map/all_to_all | solution.py:140
  130.8 6.0 %convolution_bitcast_fusion.3 = f32[1,64,1024]{2,1,0:T(8,128)S(1)} fusion(bf16[1024,4096]{1,0:T(8,128)(2,1)} %param.16, f32[8,4096]{1,0:T(8,128)S(1)} %get-tuple-element.152, f32[8,4096]{1,0:T(8,128)S(1)} %bitcast.211, f32[8,4096]{1,0:T(8,128)S(1)} %get-tuple-element.151, f32[8,4096]{1,0:T(8,128)S(1)} %bitcast.213), kind=kOutput, calls=%fused_computation.35 | convolution fusion | flops 537919488 | bytes 9175040 | tf_op jit(solution)/shard_map/dot_general | solution.py:93
  136.8 6.0 %convolution_bitcast_fusion.4 = f32[1,64,1024]{2,1,0:T(8,128)S(1)} fusion(bf16[1024,4096]{1,0:T(8,128)(2,1)} %param.16, f32[8,4096]{1,0:T(8,128)S(1)} %get-tuple-element.152, f32[8,4096]{1,0:T(8,128)S(1)} %bitcast.212, f32[8,4096]{1,0:T(8,128)S(1)} %get-tuple-element.151, f32[8,4096]{1,0:T(8,128)S(1)} %bitcast.214), kind=kOutput, calls=%fused_computation.36 | convolution fusion | flops 537919488 | bytes 9175040 | tf_op jit(solution)/shard_map/dot_general | solution.py:92
  142.9 0.8 maximum_multiply_fusion
  (69 shorter events, 5.8 us)
Async XLA Ops:
  0.0 57.5 %copy-start = (bf16[1,256,1024]{2,1,0:T(8,128)(2,1)S(1)}, bf16[1,256,1024]{2,1,0:T(8,128)(2,1)}, u32[]{:S(2)}) copy-start(bf16[1,256,1024]{2,1,0:T(8,128)(2,1)} %param.21) | copy-start | bytes 1572868
  0.0 5.9 %copy-start.1 = (bf16[1024,4096]{1,0:T(8,128)(2,1)S(1)}, bf16[1024,4096]{1,0:T(8,128)(2,1)}, u32[]{:S(2)}) copy-start(bf16[1024,4096]{1,0:T(8,128)(2,1)} %param.16) | copy-start | bytes 25165828
  0.0 5.9 %copy-start.2 = (bf16[2,64,1024]{2,1,0:T(8,128)(2,1)S(1)}, bf16[2,64,1024]{2,1,0:T(8,128)(2,1)}, u32[]{:S(2)}) copy-start(bf16[2,64,1024]{2,1,0:T(8,128)(2,1)} %param.15) | copy-start | bytes 786436
  5.9 1.6 %copy-start.6 = (f32[8,4096]{1,0:T(8,128)S(1)}, f32[8,4096]{1,0:T(8,128)}, u32[]{:S(2)}) copy-start(f32[8,4096]{1,0:T(8,128)} %param.17) | copy-start | bytes 393220
  33.8 8.8 %copy-start.3 = (f32[2,316,256]{2,0,1:T(2,128)S(1)}, f32[2,316,256]{2,0,1:T(2,128)}, u32[]{:S(2)}) copy-start(f32[2,316,256]{2,0,1:T(2,128)} %param.18) | copy-start | bytes 1941508
  34.9 7.8 %copy-start.7 = (s32[128,64]{0,1:T(8,128)S(1)}, s32[128,64]{0,1:T(8,128)}, u32[]{:S(2)}) copy-start(s32[128,64]{0,1:T(8,128)} %param.24) | copy-start | bytes 98308
  34.9 7.9 %copy-start.8 = (s32[128,64]{0,1:T(8,128)S(1)}, s32[128,64]{0,1:T(8,128)}, u32[]{:S(2)}) copy-start(s32[128,64]{0,1:T(8,128)} %param.25) | copy-start | bytes 98308
  34.9 8.1 %copy-start.4 = (f32[2,316,1,128]{3,2,1,0:T(1,128)S(1)}, f32[2,316,1,128]{3,2,1,0:T(1,128)}, u32[]{:S(2)}) copy-start(f32[2,316,1,128]{3,2,1,0:T(1,128)} %param.23) | copy-start | bytes 970756
  34.9 20.3 %all-to-all-start.1 = ((bf16[8,2,128,256]{3,2,1,0:T(8,128)(2,1)}), bf16[8,2,128,256]{3,2,1,0:T(8,128)(2,1)S(1)}, u32[]{:S(2)}, u32[]{:S(2)}) async-start(bf16[8,2,128,256]{3,2,1,0:T(8,128)(2,1)} %broadcast_in_dim.18), calls=%async_computation.1 | async-start | bytes 2097152 | tf_op jit(solution)/shard_map/all_to_all | solution.py:11
  72.2 5.5 %copy-start.5 = (f32[4,2,32,256]{3,2,0,1:T(8,128)S(1)}, f32[4,2,32,256]{3,2,0,1:T(8,128)}, u32[]{:S(2)}) copy-start(f32[4,2,32,256]{3,2,0,1:T(8,128)} %custom-call) | copy-start | bytes 786436
  73.2 43.4 %all-to-all-start.2 = ((bf16[8,2,128,256]{3,2,1,0:T(8,128)(2,1)}), bf16[8,2,128,256]{3,2,1,0:T(8,128)(2,1)}, u32[]{:S(2)}, u32[]{:S(2)}) async-start(bf16[8,2,128,256]{3,2,1,0:T(8,128)(2,1)} %copy.63), calls=%async_computation.2 | async-start | bytes 2097152 | tf_op jit(solution)/shard_map/all_to_all | solution.py:32
where the time goes:
time: 145 us; the launch traced here: 144 us
  matrix products  48.8 us (34%)
  blocking collectives  28.1 us (19%)
  other arithmetic  23.2 us (16%)
  local copies, waits for them, and re-layouts  22.3 us (15%)
  waiting for transfers between devices  11 us (8%)
  starting transfers between devices  9.7 us (7%)
    dot_general x8, matrix products, one_block(): jnp.einsum('rn,cnk->crk', source_hot, patterns, preferred_element_type=jn...  17.5 us
    all_to_all x1, blocking collectives, on_device(): lax.all_to_all(own_parents, 'dir', split_axis=2, concat_axis=1, tiled=True)  15.8 us
    all_to_all x1, blocking collectives, on_device(): lax.all_to_all(mid_in, 'dir', split_axis=1, concat_axis=2, tiled=True)  12.3 us
    all_to_all x1, waiting for transfers between devices, from_everyone(): return lax.all_to_all(copies, axis, split_axis=0, concat_axis=0, tiled=True)  11 us
    dot_general x8, matrix products, one_block(): factors = jnp.einsum('ro,cok->crk', offset_hot, operators)  9.32 us
    sub x8, other arithmetic, one_block(): real_part = jnp.sum(picked[0] * factors[0] - picked[1] * factors[1], axis=1)  8.43 us
    reduce_sum x8, other arithmetic, one_block(): imag_part = jnp.sum(picked[0] * factors[1] + picked[1] * factors[0], axis=1)  7.66 us
    dot_general x2, matrix products, adjoint_apply(): lax.dot_general(children[0], matrix, dims, preferred_element_type=jnp.flo...  6.35 us
  transfers between devices with their start and end apart: 2, of which 1 were waited for; matrix products, arithmetic and copies ran while one was open for 30% of the time, Pallas kernels for 0%

commit v1 on v0

v1 whole, which is shorter than its diff:
```python
import jax
import jax.numpy as jnp
from jax import lax
from jax.experimental import pallas as pl
from jax.experimental.pallas import tpu as pltpu
from jax.sharding import PartitionSpec as P

MESH = pl.DeviceIdType.MESH
F32 = jnp.float32
BF16 = jnp.bfloat16
VMEM = pltpu.VMEM
DMA = pltpu.SemaphoreType.DMA
PLANES = 4
SECTORS = 16
LANES = 128


def place():
    box = lax.axis_index("box")
    way = lax.axis_index("dir")
    low = box % 2
    core = way % 2
    return box // 2, way - core + low, core


def device_of(plane, sector, core):
    low = sector % 2
    return (plane * 2 + low, sector - low + core)


def sin_cos(angle):
    half = angle * 0.5
    sq = half * half
    s = sq * (-1.0 / 39916800.0) + (1.0 / 362880.0)
    s = sq * s - (1.0 / 5040.0)
    s = sq * s + (1.0 / 120.0)
    s = sq * s - (1.0 / 6.0)
    s = half + half * (sq * s)
    c = sq * (1.0 / 479001600.0) - (1.0 / 3628800.0)
    c = sq * c + (1.0 / 40320.0)
    c = sq * c - (1.0 / 720.0)
    c = sq * c + (1.0 / 24.0)
    c = sq * c - 0.5
    c = sq * c + 1.0
    return 2.0 * s * c, 1.0 - 2.0 * s * s


class Spread:
    def __init__(self, ref, send, recv):
        z, sector, core = place()
        self.ref, self.send, self.recv = ref, send, recv
        self.core = core
        self.z = z
        self.left = (z + PLANES - 1) % PLANES
        self.right = (z + 1) % PLANES
        self.far = (z + 2) % PLANES
        self.to_right = device_of(self.right, sector, core)
        self.to_left = device_of(self.left, sector, core)
        self.partner = device_of(z, sector, 1 - core)
        self.rows = ref.shape[2]

    def copy(self, plane, core, half, index, target):
        rows = self.rows
        if half is None:
            part = self.ref.at[plane, core]
        else:
            part = self.ref.at[plane, core, pl.ds(half * (rows // 2), rows // 2)]
        return pltpu.make_async_remote_copy(
            src_ref=part,
            dst_ref=part,
            send_sem=self.send.at[index],
            recv_sem=self.recv.at[index],
            device_id=target,
            device_id_type=MESH,
        )

    def start_own(self):
        self.copy(self.z, self.core, None, 0, self.to_right).start()
        self.copy(self.z, self.core, None, 1, self.to_left).start()
        self.copy(self.z, self.core, None, 4, self.partner).start()

    def forward(self):
        self.copy(self.left, self.core, None, 0, self.to_right).wait_recv()
        self.copy(self.left, self.core, 0, 2, self.to_right).start()
        self.copy(self.left, self.core, None, 5, self.partner).start()
        self.copy(self.right, self.core, None, 1, self.to_left).wait_recv()
        self.copy(self.right, self.core, 1, 3, self.to_left).start()
        self.copy(self.right, self.core, None, 6, self.partner).start()

    def forward_far(self):
        self.copy(self.far, self.core, 0, 2, self.to_right).wait_recv()
        self.copy(self.far, self.core, 1, 3, self.to_left).wait_recv()
        self.copy(self.far, self.core, None, 7, self.partner).start()

    def finish(self):
        other = 1 - self.core
        for index, plane in ((4, self.z), (5, self.left), (6, self.right), (7, self.far)):
            self.copy(plane, other, None, index, self.partner).wait_recv()
        self.copy(self.z, self.core, None, 0, self.to_right).wait_send()
        self.copy(self.z, self.core, None, 1, self.to_left).wait_send()
        self.copy(self.left, self.core, 0, 2, self.to_right).wait_send()
        self.copy(self.right, self.core, 1, 3, self.to_left).wait_send()
        for index, plane in ((4, self.z), (5, self.left), (6, self.right), (7, self.far)):
            self.copy(plane, self.core, None, index, self.partner).wait_send()


def up_kernel(
    leaf_ref,
    matrix_ref,
    shift_ref,
    trans_top_ref,
    trans_mid_ref,
    interp_top_ref,
    shift_top_ref,
    p_all,
    tp_all,
    t_all,
    trans_mid_x,
    interp_top_x,
    shift_top_x,
    weights,
    leaf_rows,
    cos_mid,
    sin_mid,
    sending,
    stage,
    piece,
    block_f32,
    top_lhs,
    top_f32,
    cos_top,
    sin_top,
    weight_sem,
    a2a_send,
    a2a_recv,
    swap_sem,
    share_send,
    share_recv,
    share_local,
    t_send,
    t_recv,
    p_send,
    p_recv,
    tp_send,
    tp_recv,
):
    z, sector, core = place()
    low = sector % 2
    own = low == core
    partner = device_of(z, sector, 1 - core)
    swap = device_of(z, sector - low + core, low)
    right = device_of((z + 1) % PLANES, sector, core)
    left = device_of((z + PLANES - 1) % PLANES, sector, core)

    def weight_copy(s):
        return pltpu.make_async_copy(
            matrix_ref.at[:, pl.ds(pl.multiple_of(s * 256, 256), 256)], weights.at[s], weight_sem.at[s]
        )

    def start_weight(k, carry):
        weight_copy((sector + 1 + k) % SECTORS).start()
        return carry

    barrier = pltpu.get_barrier_semaphore()

    def signal_peer(k, carry):
        pl.semaphore_signal(
            barrier, inc=1, device_id=device_of(z, (sector + 1 + k) % SECTORS, core), device_id_type=MESH
        )
        return carry

    lax.fori_loop(0, SECTORS - 1, signal_peer, 0)
    for device in (right, left, partner):
        pl.semaphore_signal(barrier, inc=1, device_id=device, device_id_type=MESH)

    @pl.when(jnp.logical_not(own))
    def _():
        pl.semaphore_signal(barrier, inc=1, device_id=swap, device_id_type=MESH)

    lax.fori_loop(0, SECTORS, start_weight, 0)

    offsets = trans_top_ref.shape[1]
    piece[...] = jnp.zeros_like(piece)
    half_rows = piece.shape[0] // 2
    for part in range(2):
        piece[part * half_rows : part * half_rows + offsets, :] = trans_top_ref[part].astype(BF16)

    rows = 2 * leaf_ref.shape[1]
    target = lax.broadcasted_iota(jnp.int32, (rows, rows), 0)
    source = lax.broadcasted_iota(jnp.int32, (rows, rows), 1)
    wanted = (target & 64) + ((target & 7) << 3) + ((target >> 3) & 7)
    order = (source == wanted).astype(BF16)
    both = jnp.concatenate([leaf_ref[0], leaf_ref[1]], axis=0)
    leaf_rows[...] = jnp.dot(order, both, preferred_element_type=F32).astype(BF16)

    pl.semaphore_wait(barrier, SECTORS - 1 + 3 + (low + core) % 2)

    swap_copy = pltpu.make_async_remote_copy(
        src_ref=piece,
        dst_ref=t_all.at[z, low],
        send_sem=swap_sem.at[0],
        recv_sem=swap_sem.at[1],
        device_id=swap,
        device_id_type=MESH,
    )
    shared = ((trans_mid_ref, trans_mid_x), (interp_top_ref, interp_top_x), (shift_top_ref, shift_top_x))

    def share_copy(index):
        return pltpu.make_async_remote_copy(
            src_ref=shared[index][0],
            dst_ref=shared[index][1],
            send_sem=share_send.at[index],
            recv_sem=share_recv.at[index],
            device_id=partner,
            device_id_type=MESH,
        )

    def local_copy(index):
        return pltpu.make_async_copy(shared[index][0], shared[index][1], share_local.at[index])

    @pl.when(own)
    def _():
        for index in range(3):
            share_copy(index).start()
            local_copy(index).start()
        t_all[z, core] = piece[...]

    @pl.when(jnp.logical_not(own))
    def _():
        swap_copy.start()

    sines, cosines = sin_cos(shift_ref[...])
    cos_mid[...] = cosines
    sin_mid[...] = sines

    def parents(s):
        columns = pl.ds(pl.multiple_of(s * 256, 256), 256)
        weight_copy(s).wait()
        spread = jnp.dot(leaf_rows[...], weights[s], preferred_element_type=F32)
        real_sum = jnp.zeros((8, 256), F32)
        imag_sum = jnp.zeros((8, 256), F32)
        for child in range(8):
            real = spread[child * 8 : child * 8 + 8]
            imag = spread[64 + child * 8 : 64 + child * 8 + 8]
            c = cos_mid[child : child + 1, columns]
            n = sin_mid[child : child + 1, columns]
            real_sum += real * c - imag * n
            imag_sum += real * n + imag * c
        for part in range(2):
            lanes = slice(part * LANES, part * LANES + LANES)
            stage[pl.ds(part, 8, stride=4), :] = real_sum[:, lanes]
            stage[pl.ds(2 + part, 8, stride=4), :] = imag_sum[:, lanes]
        return stage[...].astype(BF16)

    def a2a_copy(s):
        return pltpu.make_async_remote_copy(
            src_ref=sending.at[s],
            dst_ref=p_all.at[z, core, pl.ds(pl.multiple_of(sector * 32, 32), 32)],
            send_sem=a2a_send.at[s],
            recv_sem=a2a_recv.at[sector],
            device_id=device_of(z, s, core),
            device_id_type=MESH,
        )

    def arrived(s):
        return pltpu.make_async_remote_copy(
            src_ref=sending.at[s],
            dst_ref=p_all.at[z, core, pl.ds(pl.multiple_of(s * 32, 32), 32)],
            send_sem=a2a_send.at[s],
            recv_sem=a2a_recv.at[s],
            device_id=device_of(z, s, core),
            device_id_type=MESH,
        )

    def send_sector(k, carry):
        s = (sector + 1 + k) % SECTORS
        sending[s] = parents(s)
        a2a_copy(s).start()
        return carry

    t_spread = Spread(t_all, t_send, t_recv)
    p_spread = Spread(p_all, p_send, p_recv)
    tp_spread = Spread(tp_all, tp_send, tp_recv)

    lax.fori_loop(0, 6, send_sector, 0)

    @pl.when(jnp.logical_not(own))
    def _():
        swap_copy.wait()

    t_spread.start_own()
    lax.fori_loop(6, SECTORS - 1, send_sector, 0)
    p_all[z, core, pl.ds(pl.multiple_of(sector * 32, 32), 32), :] = parents(sector)
    t_spread.forward()

    def wait_sector(k, carry):
        s = (sector + 1 + k) % SECTORS
        arrived(s).wait_recv()
        return carry

    lax.fori_loop(0, SECTORS - 1, wait_sector, 0)
    p_spread.start_own()

    block_f32[...] = p_all[z, core].astype(F32)

    @pl.when(own)
    def _():
        for index in range(3):
            local_copy(index).wait()

    @pl.when(jnp.logical_not(own))
    def _():
        for index in range(3):
            share_copy(index).wait_recv()

    sines_t, cosines_t = sin_cos(shift_top_x[...])
    cos_top[...] = cosines_t
    sin_top[...] = sines_t
    for child in range(8):
        for part in range(2):
            for side in range(2):
                first = child * 4 + part * 2 + side
                a = block_f32[pl.ds(first, 8, stride=32), :]
                b = block_f32[pl.ds(256 + first, 8, stride=32), :]
                top_lhs[
                    part * 128 + child * 16 : part * 128 + child * 16 + 16, side * LANES : side * LANES + LANES
                ] = jnp.concatenate([a, b], axis=0).astype(BF16)

    def top_columns(k, carry):
        columns = pl.ds(pl.multiple_of(k * 256, 256), 256)
        spread = jnp.dot(top_lhs[...], interp_top_x[:, columns], preferred_element_type=F32)
        real_sum = jnp.zeros((16, 256), F32)
        imag_sum = jnp.zeros((16, 256), F32)
        for child in range(8):
            real = spread[child * 16 : child * 16 + 16]
            imag = spread[128 + child * 16 : 128 + child * 16 + 16]
            c = cos_top[child : child + 1, columns]
            n = sin_top[child : child + 1, columns]
            real_sum += real * c - imag * n
            imag_sum += real * n + imag * c
        for part in range(2):
            lanes = slice(part * LANES, part * LANES + LANES)
            for half in range(2):
                group = slice(half * 8, half * 8 + 8)
                top_f32[pl.ds(half * 128 + k * 2 + part, 8, stride=16), :] = real_sum[group, lanes]
                top_f32[pl.ds(half * 128 + 8 + k * 2 + part, 8, stride=16), :] = imag_sum[group, lanes]
        return carry

    lax.fori_loop(0, 4, top_columns, 0)
    tp_all[z, core] = top_f32[...].astype(BF16)
    tp_spread.start_own()
    t_spread.forward_far()
    p_spread.forward()
    tp_spread.forward()
    p_spread.forward_far()
    tp_spread.forward_far()

    def wait_sent(k, carry):
        a2a_copy((sector + 1 + k) % SECTORS).wait_send()
        return carry

    lax.fori_loop(0, SECTORS - 1, wait_sent, 0)

    @pl.when(own)
    def _():
        for index in range(3):
            share_copy(index).wait_send()

    t_spread.finish()
    p_spread.finish()
    tp_spread.finish()


def translate_kernel(
    p_all,
    tp_all,
    t_all,
    trans_mid,
    interp_top,
    shift_top,
    list_mid,
    offset_mid,
    list_top,
    offset_top,
    out,
    p_tab,
    t_tab,
    p_top,
    t_top,
    mid_sum,
    top_sum,
    child_rows,
    down,
    lists_v,
    tops_v,
    lists_w,
    tops_w,
    list_s,
    offset_s,
    list_ts,
    offset_ts,
    fetch_sem,
    index_sem,
):
    z, sector, core = place()
    mids = ((list_mid, 0, list_s), (offset_mid, 1, offset_s))
    tops = ((list_top, 0, list_ts), (offset_top, 1, offset_ts))

    def fetch_rows(k):
        low = k % 2
        row = (2 * z + low) * 128 + (k - low + core) * 8
        return [
            pltpu.make_async_copy(
                ref.at[pl.ds(pl.multiple_of(row, 8), 8)],
                lists_v.at[which, pl.ds(pl.multiple_of(k * 8, 8), 8)],
                fetch_sem.at[2 + which * SECTORS + k],
            )
            for ref, which, _ in mids
        ]

    def start_rows(k, carry):
        for copy in fetch_rows(k):
            copy.start()
        return carry

    def wait_rows(k, carry):
        for copy in fetch_rows(k):
            copy.wait()
        return carry

    fetch_tops = [pltpu.make_async_copy(ref, tops_v.at[which], fetch_sem.at[which]) for ref, which, _ in tops]
    lax.fori_loop(0, SECTORS, start_rows, 0)
    for copy in fetch_tops:
        copy.start()

    upper = lax.broadcasted_iota(jnp.int32, (8, LANES), 0) < 4

    def mid_rows(k, carry):
        plane = k // 32
        cpart = (k // 16) % 2
        s = k % 16
        low = s % 2
        first = ((2 * plane + low) * 128 + (s - low + cpart) * 8) * 8
        rows = p_all[plane, cpart, pl.ds(pl.multiple_of(s * 32, 32), 32), :].astype(F32)
        made = []
        for pair in range(4):
            v = rows[pair * 8 : pair * 8 + 8]
            r = pltpu.roll(v, 4, 0)
            made += [jnp.where(upper, v, r), jnp.where(upper, r, v)]
        p_tab[pl.ds(pl.multiple_of(first, 64), 64), :] = jnp.concatenate(made, axis=0)
        top = (2 * plane + low) * 16 + (s - low + cpart)
        p_top[pl.ds(pl.multiple_of(top * 16, 16), 16), :] = tp_all[
            plane, cpart, pl.ds(pl.multiple_of(s * 16, 16), 16), :
        ].astype(F32)
        return carry

    lax.fori_loop(0, PLANES * 2 * SECTORS, mid_rows, 0)

    def put_offsets(start, source_start):
        for part in range(2):
            for side in range(2):
                v = trans_mid[part, source_start, side * LANES : side * LANES + LANES]
                t_tab[pl.ds(start + part * 4 + side, 8, stride=8), :] = v
                t_tab[pl.ds(start + part * 4 + 2 + side, 8, stride=8), :] = v

    offsets = trans_mid.shape[1]

    def mid_offsets(k, carry):
        put_offsets(pl.multiple_of(k * 64, 64), pl.ds(pl.multiple_of(k * 8, 8), 8))
        return carry

    lax.fori_loop(0, offsets // 8, mid_offsets, 0)
    if offsets % 8:
        put_offsets((offsets - 8) * 8, slice(offsets - 8, offsets))

    def top_offsets(k, carry):
        for piece in range(8):
            for part in range(2):
                rows = t_all[
                    piece // 2, piece % 2, pl.ds(pl.multiple_of(part * 320 + k * 16, 16), 16), :
                ].astype(F32)
                for half in range(2):
                    t_top[pl.ds((k * 16 + half * 8) * 16 + part * 8 + piece, 8, stride=16), :] = rows[
                        half * 8 : half * 8 + 8
                    ]
        return carry

    lax.fori_loop(0, 20, top_offsets, 0)

    lax.fori_loop(0, SECTORS, wait_rows, 0)
    for copy in fetch_tops:
        copy.wait()
    to_smem = []
    for _, which, target in mids:
        lists_w[which] = lists_v[which] * 8
        to_smem.append(pltpu.make_async_copy(lists_w.at[which], target, index_sem.at[which]))
    for _, which, target in tops:
        tops_w[which] = tops_v[which] * 16
        to_smem.append(pltpu.make_async_copy(tops_w.at[which], target, index_sem.at[2 + which]))
    for copy in to_smem:
        copy.start()
    for copy in to_smem:
        copy.wait()

    entries = list_mid.shape[1]

    def top_box(k, carry):
        low = k % 2
        row = (2 * z + low) * 16 + (k - low + core)
        sums = [jnp.zeros((8, LANES), F32) for _ in range(4)]
        for j in range(entries):
            n = list_ts[row, j]
            o = offset_ts[row, j]
            pr = p_top[pl.ds(pl.multiple_of(n, 8), 8), :]
            pi = p_top[pl.ds(pl.multiple_of(n + 8, 8), 8), :]
            tr = t_top[pl.ds(pl.multiple_of(o, 8), 8), :]
            ti = t_top[pl.ds(pl.multiple_of(o + 8, 8), 8), :]
            sums = [sums[0] + pr * tr, sums[1] + pi * ti, sums[2] + pr * ti, sums[3] + pi * tr]
        real = (sums[0] - sums[1]).astype(BF16).astype(F32)
        imag = (sums[2] + sums[3]).astype(BF16).astype(F32)
        top_sum[pl.ds(pl.multiple_of(k * 16, 16), 8), :] = real
        top_sum[pl.ds(pl.multiple_of(k * 16 + 8, 8), 8), :] = imag
        return carry

    lax.fori_loop(0, SECTORS, top_box, 0)

    sines, cosines = sin_cos(shift_top[...])

    def children(k, carry):
        for part in range(8):
            lanes = slice(part * LANES, part * LANES + LANES)
            c = cosines[:, lanes]
            n = sines[:, lanes]
            reals = []
            imags = []
            for half in range(2):
                first = k * 32 + half * 16 + part
                real = jnp.broadcast_to(top_sum[pl.ds(first, 1), :], (8, LANES))
                imag = jnp.broadcast_to(top_sum[pl.ds(first + 8, 1), :], (8, LANES))
                reals.append(real * c + imag * n)
                imags.append(imag * c - real * n)
            at = pl.multiple_of(k * 16, 16)
            child_rows[pl.ds(at, 16), lanes] = jnp.concatenate(reals, axis=0).astype(BF16)
            child_rows[pl.ds(128 + at, 16), lanes] = jnp.concatenate(imags, axis=0).astype(BF16)
        return carry

    lax.fori_loop(0, 8, children, 0)
    scale = interp_top.shape[0] / interp_top.shape[1]
    down[...] = scale * lax.dot_general(
        child_rows[...], interp_top[...], (((1,), (1,)), ((), ())), preferred_element_type=F32
    )

    def mid_box(k, carry):
        sums = [jnp.zeros((8, LANES), F32) for _ in range(4)]
        for j in range(entries):
            p = p_tab[pl.ds(pl.multiple_of(list_s[k, j], 8), 8), :]
            t = t_tab[pl.ds(pl.multiple_of(offset_s[k, j], 8), 8), :]
            sums[j % 4] = sums[j % 4] + p * t
        mid_sum[pl.ds(pl.multiple_of(k * 8, 8), 8), :] = (sums[0] + sums[1]) + (sums[2] + sums[3])
        return carry

    lax.fori_loop(0, SECTORS * 8, mid_box, 0)

    def combine(k, carry):
        at = pl.multiple_of(k * 8, 8)
        for side in range(2):
            lanes = slice(side * LANES, side * LANES + LANES)
            real = mid_sum[pl.ds(k * 64 + side, 8, stride=8), :] - mid_sum[pl.ds(k * 64 + 6 + side, 8, stride=8), :]
            imag = mid_sum[pl.ds(k * 64 + 2 + side, 8, stride=8), :] + mid_sum[pl.ds(k * 64 + 4 + side, 8, stride=8), :]
            real = real + down[pl.ds(at, 8), lanes]
            imag = imag + down[pl.ds(pl.multiple_of(128 + k * 8, 8), 8), lanes]
            out[k, :, lanes] = jnp.concatenate([real, imag], axis=0).astype(BF16)
        return carry

    lax.fori_loop(0, SECTORS, combine, 0)


def down_kernel(
    pieces,
    matrix_ref,
    shift_ref,
    out,
    weights,
    received,
    children,
    weight_sem,
    send_sem,
    recv_sem,
):
    z, sector, core = place()
    barrier = pltpu.get_barrier_semaphore()

    def signal_peer(k, carry):
        pl.semaphore_signal(
            barrier, inc=1, device_id=device_of(z, (sector + 1 + k) % SECTORS, core), device_id_type=MESH
        )
        return carry

    lax.fori_loop(0, SECTORS - 1, signal_peer, 0)
    chunk = 256
    count = matrix_ref.shape[0] // chunk
    copies = [
        pltpu.make_async_copy(matrix_ref.at[pl.ds(k * chunk, chunk)], weights.at[pl.ds(k * chunk, chunk)], weight_sem.at[k])
        for k in range(count)
    ]
    for copy in copies:
        copy.start()
    received[sector] = pieces[sector]
    pl.semaphore_wait(barrier, SECTORS - 1)

    def out_copy(s):
        return pltpu.make_async_remote_copy(
            src_ref=pieces.at[s],
            dst_ref=received.at[sector],
            send_sem=send_sem.at[s],
            recv_sem=recv_sem.at[sector],
            device_id=device_of(z, s, core),
            device_id_type=MESH,
        )

    def in_copy(s):
        return pltpu.make_async_remote_copy(
            src_ref=pieces.at[s],
            dst_ref=received.at[s],
            send_sem=send_sem.at[s],
            recv_sem=recv_sem.at[s],
            device_id=device_of(z, s, core),
            device_id_type=MESH,
        )

    def start(k, carry):
        out_copy((sector + 1 + k) % SECTORS).start()
        return carry

    lax.fori_loop(0, SECTORS - 1, start, 0)

    def make_children(s):
        columns = pl.ds(pl.multiple_of(s * 256, 256), 256)
        n, c = sin_cos(shift_ref[:, columns])
        rows = received[s].astype(F32)
        for pair in range(4):
            reals = []
            imags = []
            for half in range(2):
                box = pair * 2 + half
                real = jnp.broadcast_to(rows[box : box + 1], (8, 256))
                imag = jnp.broadcast_to(rows[8 + box : 9 + box], (8, 256))
                reals.append(real * c + imag * n)
                imags.append(imag * c - real * n)
            children[pair * 16 : pair * 16 + 16, columns] = jnp.concatenate(reals, axis=0).astype(BF16)
            children[64 + pair * 16 : 80 + pair * 16, columns] = jnp.concatenate(imags, axis=0).astype(BF16)

    make_children(sector)

    def take(k, carry):
        s = (sector + 1 + k) % SECTORS
        in_copy(s).wait_recv()
        make_children(s)
        return carry

    lax.fori_loop(0, SECTORS - 1, take, 0)
    scale = matrix_ref.shape[0] / matrix_ref.shape[1]
    for copy in copies:
        copy.wait()

    def columns_out(k, carry):
        at = pl.ds(pl.multiple_of(k * chunk, chunk), chunk)
        part = scale * lax.dot_general(
            children[...], weights[at, :], (((1,), (1,)), ((), ())), preferred_element_type=F32
        )
        out[0, :, at] = part[:64]
        out[1, :, at] = part[64:]
        return carry

    lax.fori_loop(0, count, columns_out, 0)

    def wait_sent(k, carry):
        out_copy((sector + 1 + k) % SECTORS).wait_send()
        return carry

    lax.fori_loop(0, SECTORS - 1, wait_sent, 0)


def in_vmem(count):
    return [pl.BlockSpec(memory_space=VMEM)] * count


def in_hbm(count):
    return [pl.BlockSpec(memory_space=pltpu.HBM)] * count


def anywhere(count):
    return [pl.BlockSpec(memory_space=pl.ANY)] * count


def on_device(
    leaf_out,
    interp_mid,
    shift_mid,
    trans_mid,
    list_mid,
    offset_mid,
    interp_top,
    shift_top,
    trans_top,
    list_top,
    offset_top,
):
    offsets = trans_mid.shape[1]
    padded = 320
    trans_top = trans_top[:, :, 0, :]
    interp_top = interp_top[0]
    shift_top = shift_top[:, 0, :]
    rows = 2 * leaf_out.shape[1]
    shapes = (
        jax.ShapeDtypeStruct((PLANES, 2, 512, LANES), BF16),
        jax.ShapeDtypeStruct((PLANES, 2, 256, LANES), BF16),
        jax.ShapeDtypeStruct((PLANES, 2, 2 * padded, LANES), BF16),
        jax.ShapeDtypeStruct(trans_mid.shape, F32),
        jax.ShapeDtypeStruct(interp_top.shape, BF16),
        jax.ShapeDtypeStruct(shift_top.shape, F32),
    )
    gathered = pl.pallas_call(
        up_kernel,
        out_shape=shapes,
        in_specs=in_vmem(1) + in_hbm(1) + in_vmem(2) + anywhere(3),
        out_specs=in_vmem(6),
        scratch_shapes=[
            VMEM((SECTORS, interp_mid.shape[0], 256), BF16),
            VMEM((rows, interp_mid.shape[0]), BF16),
            VMEM(shift_mid.shape, F32),
            VMEM(shift_mid.shape, F32),
            VMEM((SECTORS, 32, LANES), BF16),
            VMEM((32, LANES), F32),
            VMEM((2 * padded, LANES), BF16),
            VMEM((512, LANES), F32),
            VMEM((256, 256), BF16),
            VMEM((256, LANES), F32),
            VMEM(shift_top.shape, F32),
            VMEM(shift_top.shape, F32),
            DMA((SECTORS,)),
            DMA((SECTORS,)),
            DMA((SECTORS,)),
            DMA((2,)),
            DMA((3,)),
            DMA((3,)),
            DMA((3,)),
            DMA((8,)),
            DMA((8,)),
            DMA((8,)),
            DMA((8,)),
            DMA((8,)),
            DMA((8,)),
        ],
        compiler_params=pltpu.CompilerParams(
            collective_id=0, has_side_effects=True, vmem_limit_bytes=24 * 1024 * 1024
        ),
        name="up",
    )(leaf_out, interp_mid, shift_mid, trans_top, trans_mid, interp_top, shift_top)

    pieces = pl.pallas_call(
        translate_kernel,
        out_shape=jax.ShapeDtypeStruct((SECTORS, 16, 256), BF16),
        in_specs=in_vmem(6) + anywhere(4),
        out_specs=pl.BlockSpec(memory_space=VMEM),
        scratch_shapes=[
            VMEM((1024 * 8, LANES), F32),
            VMEM((padded * 8, LANES), F32),
            VMEM((128 * 16, LANES), F32),
            VMEM((padded * 16, LANES), F32),
            VMEM((128 * 8, LANES), F32),
            VMEM((16 * 16, LANES), F32),
            VMEM((256, 1024), BF16),
            VMEM((256, 256), F32),
            VMEM((2, 128, list_mid.shape[1]), jnp.int32),
            VMEM((2, 128, list_mid.shape[1]), jnp.int32),
            VMEM((2, 128, list_mid.shape[1]), jnp.int32),
            VMEM((2, 128, list_mid.shape[1]), jnp.int32),
            pltpu.SMEM((128, list_mid.shape[1]), jnp.int32),
            pltpu.SMEM((128, list_mid.shape[1]), jnp.int32),
            pltpu.SMEM((128, list_mid.shape[1]), jnp.int32),
            pltpu.SMEM((128, list_mid.shape[1]), jnp.int32),
            DMA((2 + 2 * SECTORS,)),
            DMA((4,)),
        ],
        compiler_params=pltpu.CompilerParams(vmem_limit_bytes=24 * 1024 * 1024),
        name="translate",
    )(*gathered, list_mid, offset_mid, list_top, offset_top)

    return pl.pallas_call(
        down_kernel,
        out_shape=jax.ShapeDtypeStruct(leaf_out.shape, F32),
        in_specs=in_vmem(1) + in_hbm(1) + in_vmem(1),
        out_specs=pl.BlockSpec(memory_space=VMEM),
        scratch_shapes=[
            VMEM(interp_mid.shape, BF16),
            VMEM((SECTORS, 16, 256), BF16),
            VMEM((rows, interp_mid.shape[1]), BF16),
            DMA((4,)),
            DMA((SECTORS,)),
            DMA((SECTORS,)),
        ],
        compiler_params=pltpu.CompilerParams(
            collective_id=1, has_side_effects=True, vmem_limit_bytes=20 * 1024 * 1024
        ),
        name="down",
    )(pieces, interp_mid, shift_mid)


def solution(mesh):
    return jax.shard_map(
        on_device,
        mesh=mesh,
        in_specs=(
            P(None, ("box", "dir"), None),
            P(),
            P(),
            P(None, None, "dir"),
            P(),
            P(),
            P("dir", None, None),
            P(None, "dir", None),
            P(None, None, "dir", "box"),
            P(),
            P(),
        ),
        out_specs=P(None, ("box", "dir"), None),
        check_vma=False,
    )
```

time: 145 us -> 101 us (0.70)
  Pallas kernels: 0 us -> 73.8 us
  matrix products: 48.8 us -> 0 us
  blocking collectives: 28.1 us -> 0 us
  other arithmetic: 23.2 us -> 0 us
  waiting for transfers between devices: 11 us -> 0 us
  starting transfers between devices: 9.7 us -> 0 us
  local copies, waits for them, and re-layouts: 22.3 us -> 26.3 us
    pallas_call x0 -> x3, Pallas kernels: none -> 73.8 us  [the longest x1 32.6 us: on_device(): pl.pallas_call(translate_kernel, out_shape=jax.ShapeDtypeStruct((SECTORS,...]
    dot_general x28 -> x0, matrix products: 48.8 us -> none  [the longest x8 17.5 us: one_block(): jnp.einsum('rn,cnk->crk', source_hot, patterns, preferred_element_type=jn...]
    all_to_all x2 -> x0, blocking collectives: 28.1 us -> none  [the longest x1 15.8 us: on_device(): lax.all_to_all(own_parents, 'dir', split_axis=2, concat_axis=1, tiled=True)]
    unnamed x25 -> x42, local copies, waits for them, and re-layouts: 5.73 us -> 26.3 us
    reduce_sum x19 -> x0, other arithmetic: 11.1 us -> none  [the longest x8 7.66 us: one_block(): imag_part = jnp.sum(picked[0] * factors[1] + picked[1] * factors[0], axis=1)]
    all_to_all x2 -> x0, waiting for transfers between devices: 11 us -> none  [the longest x1 11 us: from_everyone(): return lax.all_to_all(copies, axis, split_axis=0, concat_axis=0, tiled=True)]
    all_to_all x2 -> x0, starting transfers between devices: 9.7 us -> none  [the longest x1 5.28 us: from_everyone(): return lax.all_to_all(copies, axis, split_axis=0, concat_axis=0, tiled=True)]
    sub x8 -> x0, other arithmetic: 8.43 us -> none  [one_block(): real_part = jnp.sum(picked[0] * factors[0] - picked[1] * factors[1], axis=1)]
  transfers between devices with their start and end apart: 2 -> 0, of which waited for: 1 -> 0; matrix products, arithmetic and copies ran while one was open for 30% -> 0% of each run, Pallas kernels for 0% -> 0%
where the time goes in v1:
time: 101 us; the launch traced here: 100 us
  Pallas kernels  73.8 us (73%)
  local copies, waits for them, and re-layouts  26.3 us (26%)
    pallas_call x1, Pallas kernels, on_device(): pl.pallas_call(translate_kernel, out_shape=jax.ShapeDtypeStruct((SECTORS,...  32.6 us
    pallas_call x1, Pallas kernels, on_device(): pl.pallas_call(up_kernel, out_shape=shapes, in_specs=in_vmem(1) + in_hbm(...  29.5 us
    unnamed x42, local copies, waits for them, and re-layouts  26.3 us
    pallas_call x1, Pallas kernels, on_device(): pl.pallas_call(down_kernel, out_shape=jax.ShapeDtypeStruct(leaf_out.shape...  11.8 us

profile of v1, /device:TPU:1, one launch (start us, length us, event | category | flops | bytes accessed | tf_op | source)
XLA Modules:
  0.0 100.3 jit_solution(10875485302489674259)
XLA Ops:
  0.0 0.0 copy-start.16
  0.0 1.2 %copy.17.trans_mid_ref = f32[2,316,256]{2,1,0:T(8,128)S(1)} copy(f32[2,316,256]{2,0,1:T(2,128)} %param.14) | data formatting | bytes 1294336 | tf_op args[3]
  1.2 1.0 copy.26
  2.2 0.8 copy.27
  3.0 0.0 copy-start
  3.0 3.4 %copy-done = bf16[1024,4096]{1,0:T(8,128)(2,1)S(1)} copy-done((bf16[1024,4096]{1,0:T(8,128)(2,1)S(1)}, bf16[1024,4096]{1,0:T(8,128)(2,1)}, u32[]{:S(2)}) %copy-start) | copy-done | bytes 8388632
  6.3 0.0 copy-start.4
  6.3 0.9 copy-done.4
  7.2 0.0 copy-start.6
  7.2 1.0 %copy-done.6 = bf16[1,256,1024]{2,1,0:T(8,128)(2,1)S(1)} copy-done((bf16[1,256,1024]{2,1,0:T(8,128)(2,1)S(1)}, bf16[1,256,1024]{2,1,0:T(8,128)(2,1)}, u32[]{:S(2)}) %copy-start.6) | copy-done | bytes 524312
  8.3 0.0 copy-start.13
  8.3 0.9 copy-done.13
  9.2 0.0 copy-start.5
  9.2 29.5 %up.1 = (bf16[4,2,512,128]{3,2,1,0:T(8,128)(2,1)S(1)}, bf16[4,2,256,128]{3,2,1,0:T(8,128)(2,1)S(1)}, bf16[4,2,640,128]{3,2,1,0:T(8,128)(2,1)S(1)}, f32[2,316,256...) custom-call(bf16[2,64,1024]{2,1,0:T(8,128)(2,1)S(1)} %copy-done.13, ...), custom_call_target="tpu_custom_call" | custom-call | tf_op jit(solution)/shard_map/up/pallas_call | solution.py:723
  38.7 0.0 copy-start.2
  38.7 0.8 copy-done.2
  39.6 0.0 copy-start.7
  39.6 0.8 copy-done.7
  40.4 0.0 copy-start.9
  40.4 0.8 copy-done.9
  41.2 0.0 copy-start.14
  41.2 0.6 copy-done.14
  41.8 0.0 copy-done.16
  41.8 0.2 copy.18.list_mid
  42.0 1.1 %copy.19.offset_mid = s32[1024,64]{1,0:T(8,128)S(1)} copy(s32[1024,64]{0,1:T(8,128)} %param.16) | data formatting | bytes 524288 | tf_op args[5]
  43.1 1.5 %copy.20.list_top = s32[128,64]{1,0:T(8,128)} copy(s32[128,64]{0,1:T(8,128)} %param.20) | data formatting | bytes 65536 | tf_op args[9]
  44.6 1.5 %copy.21.offset_top = s32[128,64]{1,0:T(8,128)} copy(s32[128,64]{0,1:T(8,128)} %param.21) | data formatting | bytes 65536 | tf_op args[10]
  46.1 0.0 copy-start.3
  46.1 1.1 %copy-done.3 = f32[2,316,256]{2,1,0:T(8,128)S(1)} copy-done((f32[2,316,256]{2,1,0:T(8,128)S(1)}, f32[2,316,256]{2,1,0:T(8,128)}, u32[]{:S(2)}) %copy-start.3) | copy-done | bytes 647192
  47.2 0.0 copy-start.8
  47.2 1.0 %copy-done.8 = bf16[4,2,256,128]{3,2,1,0:T(8,128)(2,1)S(1)} copy-done((bf16[4,2,256,128]{3,2,1,0:T(8,128)(2,1)S(1)}, bf16[4,2,256,128]{3,2,1,0:T(8,128)(2,1)}, u32[]{:S(2)}) %copy-start.8) | copy-done | bytes 524312
  48.2 0.0 copy-start.10
  48.2 1.0 %copy-done.10 = bf16[256,1024]{1,0:T(8,128)(2,1)S(1)} copy-done((bf16[256,1024]{1,0:T(8,128)(2,1)S(1)}, bf16[256,1024]{1,0:T(8,128)(2,1)}, u32[]{:S(2)}) %copy-start.10) | copy-done | bytes 524312
  49.2 0.0 copy-start.11
  49.2 0.8 copy-done.11
  50.1 0.0 copy-start.12
  50.1 0.8 copy-done.12
  50.9 0.0 copy-start.15
  50.9 0.8 copy-done.15
  51.7 32.6 %translate.1.pieces = bf16[16,16,256]{2,1,0:T(8,128)(2,1)S(1)} custom-call(bf16[4,2,512,128]{3,2,1,0:T(8,128)(2,1)S(1)} %get-tuple-element.11.p_all, bf16[4,2,256,128]{3,2,1,0:T(8,128)(2,1)S(1)} %copy-done.8, bf16[4,2,640,128]{3,2,1,0:T(8,128)(2,1)S(1)} %get-tuple-element.13.t_all, f32[2,316,256]{2,1,0:T(8,128)S(1)} %copy-done.3, ...), custom_call_target="tpu_custom_call" | custom-call | tf_op jit(solution)/shard_map/translate/pallas_call | solution.py:761
  84.3 0.0 copy-done.5
  84.3 0.0 copy-start.1
  84.3 3.4 %copy-done.1 = bf16[1024,4096]{1,0:T(8,128)(2,1)S(1)} copy-done((bf16[1024,4096]{1,0:T(8,128)(2,1)S(1)}, bf16[1024,4096]{1,0:T(8,128)(2,1)}, u32[]{:S(2)}) %copy-start.1) | copy-done | bytes 8388632
  87.7 11.8 %down.1 = f32[2,64,1024]{2,1,0:T(8,128)S(1)} custom-call(bf16[16,16,256]{2,1,0:T(8,128)(2,1)S(1)} %translate.1.pieces, bf16[1024,4096]{1,0:T(8,128)(2,1)S(1)} %copy-done.1, f32[8,4096]{1,0:T(8,128)S(1)} %copy-done.5), custom_call_target="tpu_custom_call" | custom-call | tf_op jit(solution)/shard_map/down/pallas_call | solution.py:790
  99.5 0.8 copy.29
Async XLA Ops:
  0.0 41.8 %copy-start.16 = (s32[1024,64]{0,1:T(8,128)S(1)}, s32[1024,64]{0,1:T(8,128)}, u32[]{:S(2)}) copy-start(s32[1024,64]{0,1:T(8,128)} %param.15) | copy-start | bytes 786436
  3.0 3.4 %copy-start = (bf16[1024,4096]{1,0:T(8,128)(2,1)S(1)}, bf16[1024,4096]{1,0:T(8,128)(2,1)}, u32[]{:S(2)}) copy-start(bf16[1024,4096]{1,0:T(8,128)(2,1)} %matrix_ref.3) | copy-start | bytes 25165828
  6.3 0.9 copy-start.4
  7.2 1.0 %copy-start.6 = (bf16[1,256,1024]{2,1,0:T(8,128)(2,1)S(1)}, bf16[1,256,1024]{2,1,0:T(8,128)(2,1)}, u32[]{:S(2)}) copy-start(bf16[1,256,1024]{2,1,0:T(8,128)(2,1)} %param.17) | copy-start | bytes 1572868
  8.3 0.9 copy-start.13
  9.2 75.1 %copy-start.5 = (f32[8,4096]{1,0:T(8,128)S(1)}, f32[8,4096]{1,0:T(8,128)}, u32[]{:S(2)}) copy-start(f32[8,4096]{1,0:T(8,128)} %shift_ref.3) | copy-start | bytes 393220
  38.7 0.8 copy-start.2
  39.6 0.8 copy-start.7
  40.4 0.8 copy-start.9
  41.2 0.6 copy-start.14
  46.1 1.1 %copy-start.3 = (f32[2,316,256]{2,1,0:T(8,128)S(1)}, f32[2,316,256]{2,1,0:T(8,128)}, u32[]{:S(2)}) copy-start(f32[2,316,256]{2,1,0:T(8,128)} %copy-done.2) | copy-start | bytes 1941508
  47.2 1.0 %copy-start.8 = (bf16[4,2,256,128]{3,2,1,0:T(8,128)(2,1)S(1)}, bf16[4,2,256,128]{3,2,1,0:T(8,128)(2,1)}, u32[]{:S(2)}) copy-start(bf16[4,2,256,128]{3,2,1,0:T(8,128)(2,1)} %copy-done.7) | copy-start | bytes 1572868
  48.2 1.0 %copy-start.10 = (bf16[256,1024]{1,0:T(8,128)(2,1)S(1)}, bf16[256,1024]{1,0:T(8,128)(2,1)}, u32[]{:S(2)}) copy-start(bf16[256,1024]{1,0:T(8,128)(2,1)} %copy-done.9) | copy-start | bytes 1572868
  49.2 0.8 copy-start.11
  50.1 0.8 copy-start.12
  50.9 0.8 copy-start.15
  84.3 3.4 %copy-start.1 = (bf16[1024,4096]{1,0:T(8,128)(2,1)S(1)}, bf16[1024,4096]{1,0:T(8,128)(2,1)}, u32[]{:S(2)}) copy-start(bf16[1024,4096]{1,0:T(8,128)(2,1)} %matrix_ref.3) | copy-start | bytes 25165828

commit v2 on v0

v2 whole, which is shorter than its diff:
```python
import jax
import jax.numpy as jnp
from jax import lax
from jax.experimental import pallas as pl
from jax.experimental.pallas import tpu as pltpu
from jax.sharding import PartitionSpec as P

MESH = pl.DeviceIdType.MESH
F32 = jnp.float32
BF16 = jnp.bfloat16
VMEM = pltpu.VMEM
DMA = pltpu.SemaphoreType.DMA
PLANES = 4
SECTORS = 16
LANES = 128


def place():
    box = lax.axis_index("box")
    way = lax.axis_index("dir")
    low = box % 2
    core = way % 2
    return box // 2, way - core + low, core


def device_of(plane, sector, core):
    low = sector % 2
    return (plane * 2 + low, sector - low + core)


def sin_cos(angle):
    half = angle * 0.5
    sq = half * half
    s = sq * (-1.0 / 39916800.0) + (1.0 / 362880.0)
    s = sq * s - (1.0 / 5040.0)
    s = sq * s + (1.0 / 120.0)
    s = sq * s - (1.0 / 6.0)
    s = half + half * (sq * s)
    c = sq * (1.0 / 479001600.0) - (1.0 / 3628800.0)
    c = sq * c + (1.0 / 40320.0)
    c = sq * c - (1.0 / 720.0)
    c = sq * c + (1.0 / 24.0)
    c = sq * c - 0.5
    c = sq * c + 1.0
    return 2.0 * s * c, 1.0 - 2.0 * s * s


class Spread:
    def __init__(self, ref, send, recv):
        z, sector, core = place()
        self.ref, self.send, self.recv = ref, send, recv
        self.core = core
        self.z = z
        self.left = (z + PLANES - 1) % PLANES
        self.right = (z + 1) % PLANES
        self.far = (z + 2) % PLANES
        self.to_right = device_of(self.right, sector, core)
        self.to_left = device_of(self.left, sector, core)
        self.partner = device_of(z, sector, 1 - core)
        self.rows = ref.shape[2]
        self.crossing = ((4, self.z), (5, self.left), (6, self.right), (7, self.far))

    def copy(self, plane, core, half, index, target):
        rows = self.rows
        if half is None:
            part = self.ref.at[plane, core]
        else:
            part = self.ref.at[plane, core, pl.ds(half * (rows // 2), rows // 2)]
        return pltpu.make_async_remote_copy(
            src_ref=part,
            dst_ref=part,
            send_sem=self.send.at[index],
            recv_sem=self.recv.at[index],
            device_id=target,
            device_id_type=MESH,
        )

    def start_own(self):
        self.copy(self.z, self.core, None, 0, self.to_right).start()
        self.copy(self.z, self.core, None, 1, self.to_left).start()
        self.copy(self.z, self.core, None, 4, self.partner).start()

    def forward(self):
        self.copy(self.left, self.core, None, 0, self.to_right).wait_recv()
        self.copy(self.left, self.core, 0, 2, self.to_right).start()
        self.copy(self.left, self.core, None, 5, self.partner).start()
        self.copy(self.right, self.core, None, 1, self.to_left).wait_recv()
        self.copy(self.right, self.core, 1, 3, self.to_left).start()
        self.copy(self.right, self.core, None, 6, self.partner).start()

    def forward_far(self):
        self.copy(self.far, self.core, 0, 2, self.to_right).wait_recv()
        self.copy(self.far, self.core, 1, 3, self.to_left).wait_recv()
        self.copy(self.far, self.core, None, 7, self.partner).start()

    def take(self, which):
        index, plane = self.crossing[which]
        self.copy(plane, 1 - self.core, None, index, self.partner).wait_recv()
        return plane

    def sent(self):
        self.copy(self.z, self.core, None, 0, self.to_right).wait_send()
        self.copy(self.z, self.core, None, 1, self.to_left).wait_send()
        self.copy(self.left, self.core, 0, 2, self.to_right).wait_send()
        self.copy(self.right, self.core, 1, 3, self.to_left).wait_send()
        for index, plane in self.crossing:
            self.copy(plane, self.core, None, index, self.partner).wait_send()


def kernel(
    leaf_ref,
    matrix_ref,
    shift_mid_ref,
    trans_top_ref,
    trans_mid_ref,
    interp_top_ref,
    shift_top_ref,
    list_mid_ref,
    offset_mid_ref,
    list_top_ref,
    offset_top_ref,
    out_ref,
    leaf,
    weights,
    shift_mid,
    trans_top,
    trans_mid,
    interp_top,
    shift_top,
    lists_mid,
    lists_top,
    list_s,
    offset_s,
    list_ts,
    offset_ts,
    p_all,
    tp_all,
    t_all,
    leaf_rows,
    cos_mid,
    sin_mid,
    sending,
    stage,
    piece,
    block_f32,
    top_lhs,
    top_f32,
    cos_top,
    sin_top,
    p_tab,
    t_tab,
    p_top,
    t_top,
    mid_sum,
    top_sum,
    child_rows,
    down,
    pieces,
    received,
    children,
    total,
    weight_sem,
    load_sem,
    index_sem,
    a2a_send,
    a2a_recv,
    swap_sem,
    share_send,
    share_recv,
    t_send,
    t_recv,
    p_send,
    p_recv,
    tp_send,
    tp_recv,
    back_send,
    back_recv,
    out_sem,
):
    z, sector, core = place()
    low = sector % 2
    own = low == core
    partner = device_of(z, sector, 1 - core)
    swap = device_of(z, sector - low + core, low)
    right = device_of((z + 1) % PLANES, sector, core)
    left = device_of((z + PLANES - 1) % PLANES, sector, core)
    t_spread = Spread(t_all, t_send, t_recv)
    p_spread = Spread(p_all, p_send, p_recv)
    tp_spread = Spread(tp_all, tp_send, tp_recv)

    def nth(k):
        return (sector + 1 + k) % SECTORS

    def to_sector(s):
        return device_of(z, s, core)

    barrier = pltpu.get_barrier_semaphore()

    def signal_peer(k, carry):
        pl.semaphore_signal(barrier, inc=1, device_id=to_sector(nth(k)), device_id_type=MESH)
        return carry

    lax.fori_loop(0, SECTORS - 1, signal_peer, 0)
    for device in (right, left, partner):
        pl.semaphore_signal(barrier, inc=1, device_id=device, device_id_type=MESH)

    @pl.when(jnp.logical_not(own))
    def _():
        pl.semaphore_signal(barrier, inc=1, device_id=swap, device_id_type=MESH)

    slab = pl.ds(pl.multiple_of(z * 256, 256), 256)
    loads = [
        pltpu.make_async_copy(source, target, load_sem.at[index])
        for index, (source, target) in enumerate(
            (
                (leaf_ref, leaf),
                (trans_top_ref, trans_top),
                (shift_mid_ref, shift_mid),
                (list_mid_ref.at[:, slab], lists_mid.at[0]),
                (offset_mid_ref.at[:, slab], lists_mid.at[1]),
                (list_top_ref, lists_top.at[0]),
                (offset_top_ref, lists_top.at[1]),
            )
        )
    ]
    for copy in loads[:3]:
        copy.start()

    def weight_copy(s):
        return pltpu.make_async_copy(
            matrix_ref.at[:, pl.ds(pl.multiple_of(s * 256, 256), 256)], weights.at[s], weight_sem.at[s]
        )

    def start_weight(k, carry):
        weight_copy(nth(k)).start()
        return carry

    lax.fori_loop(0, SECTORS, start_weight, 0)
    for copy in loads[3:]:
        copy.start()

    loads[0].wait()
    rows = 2 * leaf.shape[1]
    target = lax.broadcasted_iota(jnp.int32, (rows, rows), 0)
    source = lax.broadcasted_iota(jnp.int32, (rows, rows), 1)
    wanted = (target & 64) + ((target & 7) << 3) + ((target >> 3) & 7)
    order = (source == wanted).astype(BF16)
    both = jnp.concatenate([leaf[0], leaf[1]], axis=0)
    leaf_rows[...] = jnp.dot(order, both, preferred_element_type=F32).astype(BF16)

    loads[1].wait()
    used = trans_top.shape[0]
    piece[0:used, :] = trans_top[...].astype(BF16)
    piece[used:, :] = jnp.zeros((piece.shape[0] - used, LANES), BF16)

    pl.semaphore_wait(barrier, SECTORS - 1 + 3 + (low + core) % 2)

    swap_copy = pltpu.make_async_remote_copy(
        src_ref=piece,
        dst_ref=t_all.at[z, low],
        send_sem=swap_sem.at[0],
        recv_sem=swap_sem.at[1],
        device_id=swap,
        device_id_type=MESH,
    )
    shared = ((trans_mid_ref, trans_mid), (interp_top_ref, interp_top), (shift_top_ref, shift_top))

    def share_copy(index):
        return pltpu.make_async_remote_copy(
            src_ref=shared[index][0],
            dst_ref=shared[index][1],
            send_sem=share_send.at[index],
            recv_sem=share_recv.at[index],
            device_id=partner,
            device_id_type=MESH,
        )

    def local_copy(index):
        return pltpu.make_async_copy(shared[index][0], shared[index][1], share_recv.at[index])

    @pl.when(own)
    def _():
        for index in range(3):
            share_copy(index).start()
            local_copy(index).start()
        t_all[z, core] = piece[...]

    @pl.when(jnp.logical_not(own))
    def _():
        swap_copy.start()

    loads[2].wait()
    sines, cosines = sin_cos(shift_mid[...])
    cos_mid[...] = cosines
    sin_mid[...] = sines

    def parents(s, slot):
        columns = pl.ds(pl.multiple_of(s * 256, 256), 256)
        weight_copy(s).wait()
        spread = jnp.dot(leaf_rows[...], weights[s], preferred_element_type=F32)
        real_sum = jnp.zeros((8, 256), F32)
        imag_sum = jnp.zeros((8, 256), F32)
        for child in range(8):
            real = spread[child * 8 : child * 8 + 8]
            imag = spread[64 + child * 8 : 64 + child * 8 + 8]
            c = cos_mid[child : child + 1, columns]
            n = sin_mid[child : child + 1, columns]
            real_sum += real * c - imag * n
            imag_sum += real * n + imag * c
        for part in range(2):
            lanes = slice(part * LANES, part * LANES + LANES)
            stage[pl.ds(slot * 32 + part, 8, stride=4), :] = real_sum[:, lanes]
            stage[pl.ds(slot * 32 + 2 + part, 8, stride=4), :] = imag_sum[:, lanes]
        return stage[slot * 32 : slot * 32 + 32, :].astype(BF16)

    def rows_of(s):
        return p_all.at[z, core, pl.ds(pl.multiple_of(s * 32, 32), 32)]

    def a2a_copy(s, landing):
        return pltpu.make_async_remote_copy(
            src_ref=sending.at[s],
            dst_ref=rows_of(landing),
            send_sem=a2a_send.at[s],
            recv_sem=a2a_recv.at[landing],
            device_id=to_sector(s),
            device_id_type=MESH,
        )

    def send_pair(k, carry):
        first, second = nth(2 * k), nth(2 * k + 1)
        sending[first] = parents(first, 0)
        sending[second] = parents(second, 1)
        a2a_copy(first, sector).start()
        a2a_copy(second, sector).start()
        return carry

    lax.fori_loop(0, 3, send_pair, 0)

    @pl.when(jnp.logical_not(own))
    def _():
        swap_copy.wait()

    t_spread.start_own()
    lax.fori_loop(3, 7, send_pair, 0)
    last = nth(SECTORS - 2)
    sending[last] = parents(last, 0)
    a2a_copy(last, sector).start()
    p_all[z, core, pl.ds(pl.multiple_of(sector * 32, 32), 32), :] = parents(sector, 1)
    t_spread.forward()

    for copy in loads[3:]:
        copy.wait()
    to_smem = [
        pltpu.make_async_copy(source, target, index_sem.at[index])
        for index, (source, target) in enumerate(
            (
                (lists_mid.at[0], list_s),
                (lists_mid.at[1], offset_s),
                (lists_top.at[0], list_ts),
                (lists_top.at[1], offset_ts),
            )
        )
    ]
    for copy in to_smem:
        copy.start()

    @pl.when(own)
    def _():
        for index in range(3):
            local_copy(index).wait()

    @pl.when(jnp.logical_not(own))
    def _():
        for index in range(3):
            share_copy(index).wait_recv()

    offsets = trans_mid.shape[0] // 4
    t_rows = t_tab.reshape(offsets * 8, LANES)

    def put_offsets(first, row):
        for quarter, places in enumerate(((0, 2), (4, 6), (1, 3), (5, 7))):
            v = trans_mid[pl.ds(first + quarter, 8, stride=4), :]
            for at in places:
                t_rows[pl.ds(row + at, 8, stride=8), :] = v

    def mid_offsets(k, carry):
        put_offsets(pl.multiple_of(k * 32, 32), pl.multiple_of(k * 64, 64))
        return carry

    lax.fori_loop(0, offsets // 8, mid_offsets, 0)
    if offsets % 8:
        put_offsets((offsets - 8) * 4, (offsets - 8) * 8)

    sines_t, cosines_t = sin_cos(shift_top[...])
    cos_top[...] = cosines_t
    sin_top[...] = sines_t

    def wait_sector(k, carry):
        s = nth(k)
        a2a_copy(s, s).wait_recv()
        return carry

    lax.fori_loop(0, SECTORS - 1, wait_sector, 0)
    p_spread.start_own()

    block_f32[...] = p_all[z, core].astype(F32)
    for child in range(8):
        for part in range(2):
            for side in range(2):
                first = child * 4 + part * 2 + side
                a = block_f32[pl.ds(first, 8, stride=32), :]
                b = block_f32[pl.ds(256 + first, 8, stride=32), :]
                top_lhs[
                    part * 128 + child * 16 : part * 128 + child * 16 + 16, side * LANES : side * LANES + LANES
                ] = jnp.concatenate([a, b], axis=0).astype(BF16)

    def top_columns(k, carry):
        columns = pl.ds(pl.multiple_of(k * 256, 256), 256)
        spread = jnp.dot(top_lhs[...], interp_top[:, columns], preferred_element_type=F32)
        for part in range(2):
            lanes = slice(part * LANES, part * LANES + LANES)
            group = k * 2 + part
            real_sum = jnp.zeros((16, LANES), F32)
            imag_sum = jnp.zeros((16, LANES), F32)
            for child in range(8):
                real = spread[child * 16 : child * 16 + 16, lanes]
                imag = spread[128 + child * 16 : 128 + child * 16 + 16, lanes]
                c = cos_top[pl.ds(child * 8 + group, 1), :]
                n = sin_top[pl.ds(child * 8 + group, 1), :]
                real_sum += real * c - imag * n
                imag_sum += real * n + imag * c
            for half in range(2):
                boxes = slice(half * 8, half * 8 + 8)
                top_f32[pl.ds(half * 128 + group, 8, stride=16), :] = real_sum[boxes]
                top_f32[pl.ds(half * 128 + 8 + group, 8, stride=16), :] = imag_sum[boxes]
        return carry

    lax.fori_loop(0, 4, top_columns, 0)
    tp_all[z, core] = top_f32[...].astype(BF16)
    tp_spread.start_own()

    upper = lax.broadcasted_iota(jnp.int32, (8, LANES), 0) < 4

    def mid_table(plane, side):
        def one(s, carry):
            odd = s % 2
            first = (2 * plane + odd) * 128 + (s - odd + side) * 8
            found = p_all[plane, side, pl.ds(pl.multiple_of(s * 32, 32), 32), :].astype(F32)
            for pair in range(4):
                v = found[pair * 8 : pair * 8 + 8]
                r = pltpu.roll(v, 4, 0)
                p_tab[first + pair * 2] = jnp.where(upper, v, r)
                p_tab[first + pair * 2 + 1] = jnp.where(upper, r, v)
            return carry

        lax.fori_loop(0, SECTORS, one, 0)

    def top_table(plane, side):
        def one(s, carry):
            odd = s % 2
            found = tp_all[plane, side, pl.ds(pl.multiple_of(s * 16, 16), 16), :].astype(F32)
            first = (2 * plane + odd) * 16 + (s - odd + side)
            p_top[first, 0] = found[:8]
            p_top[first, 1] = found[8:]
            return carry

        lax.fori_loop(0, SECTORS, one, 0)

    def offset_table(plane, side):
        at = plane * 2 + side
        t_rows = t_top.reshape(t_top.shape[0] * 8, LANES)

        def one(k, carry):
            found = t_all[plane, side, pl.ds(pl.multiple_of(k * 16, 16), 16), :].astype(F32)
            for half in range(2):
                t_rows[pl.ds(k * 128 + half * 64 + at, 8, stride=8), :] = found[half * 8 : half * 8 + 8]
            return carry

        lax.fori_loop(0, t_all.shape[2] // 16, one, 0)

    mid_table(z, core)
    top_table(z, core)
    t_spread.forward_far()
    offset_table(z, core)
    offset_table(t_spread.left, core)
    offset_table(t_spread.right, core)
    p_spread.forward()
    tp_spread.forward()
    mid_table(p_spread.left, core)
    mid_table(p_spread.right, core)
    offset_table(t_spread.far, core)
    for which in range(3):
        mid_table(p_spread.take(which), 1 - core)
    p_spread.forward_far()
    tp_spread.forward_far()
    mid_table(p_spread.far, core)
    for which in range(4):
        offset_table(t_spread.take(which), 1 - core)
    mid_table(p_spread.take(3), 1 - core)
    for copy in to_smem:
        copy.wait()

    entries = list_mid_ref.shape[0]

    def mid_box(k, carry):
        s = k // 8
        odd = s % 2
        column = odd * 128 + (s - odd + core) * 8 + k % 8
        kept = jnp.zeros((8, LANES), F32)
        for j in range(entries):
            p = p_tab[list_s[j, column]]
            t = t_tab[offset_s[j, column]]
            kept = kept + p * t
        mid_sum[pl.ds(pl.multiple_of(k * 8, 8), 8), :] = kept
        return carry

    lax.fori_loop(0, SECTORS * 8, mid_box, 0)

    for plane in (tp_spread.left, tp_spread.right, tp_spread.far):
        top_table(plane, core)
    for which in range(4):
        top_table(tp_spread.take(which), 1 - core)

    behind = trans_top_ref.shape[0] // 2

    def top_box(k, carry):
        odd = k % 2
        column = (2 * z + odd) * 16 + (k - odd + core)
        sums = [jnp.zeros((8, LANES), F32) for _ in range(4)]
        for j in range(entries):
            n = list_ts[j, column]
            o = offset_ts[j, column]
            pr = p_top[n, 0]
            pi = p_top[n, 1]
            tr = t_top[o]
            ti = t_top[o + behind]
            sums = [sums[0] + pr * tr, sums[1] + pi * ti, sums[2] + pr * ti, sums[3] + pi * tr]
        real = (sums[0] - sums[1]).astype(BF16).astype(F32)
        imag = (sums[2] + sums[3]).astype(BF16).astype(F32)
        top_sum[pl.ds(pl.multiple_of(k * 16, 16), 8), :] = real
        top_sum[pl.ds(pl.multiple_of(k * 16 + 8, 8), 8), :] = imag
        return carry

    lax.fori_loop(0, SECTORS, top_box, 0)

    def top_children(part, carry):
        lanes = pl.ds(pl.multiple_of(part * LANES, LANES), LANES)
        c = cos_top[pl.ds(part, 8, stride=8), :]
        n = sin_top[pl.ds(part, 8, stride=8), :]
        for pair in range(8):
            reals = []
            imags = []
            for half in range(2):
                first = pair * 32 + half * 16
                real = jnp.broadcast_to(top_sum[pl.ds(first + part, 1), :], (8, LANES))
                imag = jnp.broadcast_to(top_sum[pl.ds(first + 8 + part, 1), :], (8, LANES))
                reals.append(real * c + imag * n)
                imags.append(imag * c - real * n)
            child_rows[pair * 16 : pair * 16 + 16, lanes] = jnp.concatenate(reals, axis=0).astype(BF16)
            child_rows[128 + pair * 16 : 144 + pair * 16, lanes] = jnp.concatenate(imags, axis=0).astype(BF16)
        return carry

    lax.fori_loop(0, 8, top_children, 0)
    scale = interp_top.shape[0] / interp_top.shape[1]
    down[...] = scale * lax.dot_general(
        child_rows[...], interp_top[...], (((1,), (1,)), ((), ())), preferred_element_type=F32
    )

    def back_copy(s, landing):
        return pltpu.make_async_remote_copy(
            src_ref=pieces.at[s],
            dst_ref=received.at[landing],
            send_sem=back_send.at[s],
            recv_sem=back_recv.at[landing],
            device_id=to_sector(s),
            device_id_type=MESH,
        )

    def combine(k):
        at = pl.multiple_of(k * 8, 8)
        sides = []
        for side in range(2):
            lanes = slice(side * LANES, side * LANES + LANES)
            parts = [mid_sum[pl.ds(k * 64 + side + 2 * quarter, 8, stride=8), :] for quarter in range(4)]
            real = (parts[0] - parts[3]) + down[pl.ds(at, 8), lanes]
            imag = (parts[1] + parts[2]) + down[pl.ds(pl.multiple_of(128 + k * 8, 8), 8), lanes]
            sides.append(jnp.concatenate([real, imag], axis=0).astype(BF16))
        return jnp.concatenate(sides, axis=1)

    def send_back(k, carry):
        s = nth(k)
        pieces[s] = combine(s)
        back_copy(s, sector).start()
        return carry

    lax.fori_loop(0, SECTORS - 1, send_back, 0)
    received[sector] = combine(sector)
    total[...] = jnp.zeros_like(total)

    def finish_sector(s):
        columns = pl.ds(pl.multiple_of(s * 256, 256), 256)
        c = cos_mid[:, columns]
        n = sin_mid[:, columns]
        found = received[s].astype(F32)
        for pair in range(4):
            reals = []
            imags = []
            for half in range(2):
                box = pair * 2 + half
                real = jnp.broadcast_to(found[box : box + 1], (8, 256))
                imag = jnp.broadcast_to(found[8 + box : 9 + box], (8, 256))
                reals.append(real * c + imag * n)
                imags.append(imag * c - real * n)
            children[pair * 16 : pair * 16 + 16, :] = jnp.concatenate(reals, axis=0).astype(BF16)
            children[64 + pair * 16 : 80 + pair * 16, :] = jnp.concatenate(imags, axis=0).astype(BF16)
        total[...] += lax.dot_general(
            children[...], weights[s], (((1,), (1,)), ((), ())), preferred_element_type=F32
        )

    finish_sector(sector)

    def take_back(k, carry):
        s = nth(k)
        back_copy(s, s).wait_recv()
        finish_sector(s)
        return carry

    lax.fori_loop(0, SECTORS - 1, take_back, 0)
    total[...] = total[...] * (matrix_ref.shape[0] / matrix_ref.shape[1])
    half_rows = total.shape[0] // 2
    outs = [
        pltpu.make_async_copy(total.at[pl.ds(part * half_rows, half_rows)], out_ref.at[part], out_sem.at[part])
        for part in range(2)
    ]
    for copy in outs:
        copy.start()

    def wait_sent(k, carry):
        s = nth(k)
        a2a_copy(s, sector).wait_send()
        back_copy(s, sector).wait_send()
        return carry

    lax.fori_loop(0, SECTORS - 1, wait_sent, 0)

    @pl.when(own)
    def _():
        for index in range(3):
            share_copy(index).wait_send()

    for each in (t_spread, p_spread, tp_spread):
        each.sent()
    for copy in outs:
        copy.wait()


def on_device(
    leaf_out,
    interp_mid,
    shift_mid,
    trans_mid,
    list_mid,
    offset_mid,
    interp_top,
    shift_top,
    trans_top,
    list_top,
    offset_top,
):
    offsets = trans_mid.shape[1]
    entries = list_mid.shape[1]
    rows = 2 * leaf_out.shape[1]
    operands = (
        leaf_out,
        interp_mid,
        shift_mid,
        trans_top.reshape(2 * offsets, LANES),
        jnp.transpose(trans_mid.reshape(2, offsets, 2, LANES), (1, 2, 0, 3)).reshape(4 * offsets, LANES),
        interp_top[0],
        shift_top.reshape(64, LANES),
        list_mid.T,
        offset_mid.T,
        list_top.T,
        offset_top.T,
    )
    padded = 640
    return pl.pallas_call(
        kernel,
        out_shape=jax.ShapeDtypeStruct(leaf_out.shape, F32),
        in_specs=[pl.BlockSpec(memory_space=pltpu.HBM)] * len(operands),
        out_specs=pl.BlockSpec(memory_space=pltpu.HBM),
        scratch_shapes=[
            VMEM(leaf_out.shape, BF16),
            VMEM((SECTORS, interp_mid.shape[0], 256), BF16),
            VMEM(shift_mid.shape, F32),
            VMEM((2 * offsets, LANES), F32),
            VMEM((4 * offsets, LANES), F32),
            VMEM((256, 1024), BF16),
            VMEM((64, LANES), F32),
            VMEM((2, entries, 256), jnp.int32),
            VMEM((2, entries, 128), jnp.int32),
            pltpu.SMEM((entries, 256), jnp.int32),
            pltpu.SMEM((entries, 256), jnp.int32),
            pltpu.SMEM((entries, 128), jnp.int32),
            pltpu.SMEM((entries, 128), jnp.int32),
            VMEM((PLANES, 2, 512, LANES), BF16),
            VMEM((PLANES, 2, 256, LANES), BF16),
            VMEM((PLANES, 2, padded, LANES), BF16),
            VMEM((rows, interp_mid.shape[0]), BF16),
            VMEM(shift_mid.shape, F32),
            VMEM(shift_mid.shape, F32),
            VMEM((SECTORS, 32, LANES), BF16),
            VMEM((64, LANES), F32),
            VMEM((padded, LANES), BF16),
            VMEM((512, LANES), F32),
            VMEM((256, 256), BF16),
            VMEM((256, LANES), F32),
            VMEM((64, LANES), F32),
            VMEM((64, LANES), F32),
            VMEM((1024, 8, LANES), F32),
            VMEM((offsets, 8, LANES), F32),
            VMEM((128, 2, 8, LANES), F32),
            VMEM((padded, 8, LANES), F32),
            VMEM((128 * 8, LANES), F32),
            VMEM((16 * 16, LANES), F32),
            VMEM((256, 1024), BF16),
            VMEM((256, 256), F32),
            VMEM((SECTORS, 16, 256), BF16),
            VMEM((SECTORS, 16, 256), BF16),
            VMEM((rows, 256), BF16),
            VMEM((rows, interp_mid.shape[0]), F32),
            DMA((SECTORS,)),
            DMA((7,)),
            DMA((4,)),
            DMA((SECTORS,)),
            DMA((SECTORS,)),
            DMA((2,)),
            DMA((3,)),
            DMA((3,)),
            DMA((8,)),
            DMA((8,)),
            DMA((8,)),
            DMA((8,)),
            DMA((8,)),
            DMA((8,)),
            DMA((SECTORS,)),
            DMA((SECTORS,)),
            DMA((2,)),
        ],
        compiler_params=pltpu.CompilerParams(
            collective_id=0, has_side_effects=True, vmem_limit_bytes=60 * 1024 * 1024
        ),
        name="far_field",
    )(*operands)


def solution(mesh):
    return jax.shard_map(
        on_device,
        mesh=mesh,
        in_specs=(
            P(None, ("box", "dir"), None),
            P(),
            P(),
            P(None, None, "dir"),
            P(),
            P(),
            P("dir", None, None),
            P(None, "dir", None),
            P(None, None, "dir", "box"),
            P(),
            P(),
        ),
        out_specs=P(None, ("box", "dir"), None),
        check_vma=False,
    )
```

time: 145 us -> 64.6 us (0.45)
  Pallas kernels: 0 us -> 61.9 us
  matrix products: 48.8 us -> 0 us
  blocking collectives: 28.1 us -> 0 us
  other arithmetic: 23.2 us -> 0 us
  local copies, waits for them, and re-layouts: 22.3 us -> 1.89 us
  waiting for transfers between devices: 11 us -> 0 us
  starting transfers between devices: 9.7 us -> 0 us
    pallas_call x0 -> x1, Pallas kernels: none -> 61.9 us  [on_device(): pl.pallas_call(kernel, out_shape=jax.ShapeDtypeStruct(leaf_out.shape, F32...]
    dot_general x28 -> x0, matrix products: 48.8 us -> none  [the longest x8 17.5 us: one_block(): jnp.einsum('rn,cnk->crk', source_hot, patterns, preferred_element_type=jn...]
    all_to_all x2 -> x0, blocking collectives: 28.1 us -> none  [the longest x1 15.8 us: on_device(): lax.all_to_all(own_parents, 'dir', split_axis=2, concat_axis=1, tiled=True)]
    reduce_sum x19 -> x0, other arithmetic: 11.1 us -> none  [the longest x8 7.66 us: one_block(): imag_part = jnp.sum(picked[0] * factors[1] + picked[1] * factors[0], axis=1)]
    all_to_all x2 -> x0, waiting for transfers between devices: 11 us -> none  [the longest x1 11 us: from_everyone(): return lax.all_to_all(copies, axis, split_axis=0, concat_axis=0, tiled=True)]
    all_to_all x2 -> x0, starting transfers between devices: 9.7 us -> none  [the longest x1 5.28 us: from_everyone(): return lax.all_to_all(copies, axis, split_axis=0, concat_axis=0, tiled=True)]
    sub x8 -> x0, other arithmetic: 8.43 us -> none  [one_block(): real_part = jnp.sum(picked[0] * factors[0] - picked[1] * factors[1], axis=1)]
    dynamic_slice x11 -> x0, local copies, waits for them, and re-layouts: 4.22 us -> none  [the longest x8 3.25 us: complex_translate(): blocks = lax.map(one_block, (source_blocks, offset_blocks))]
  transfers between devices with their start and end apart: 2 -> 0, of which waited for: 1 -> 0; matrix products, arithmetic and copies ran while one was open for 30% -> 0% of each run, Pallas kernels for 0% -> 0%
where the time goes in v2:
time: 64.6 us; the launch traced here: 63.8 us
  Pallas kernels  61.9 us (96%)
  local copies, waits for them, and re-layouts  1.89 us (3%)
    pallas_call x1, Pallas kernels, on_device(): pl.pallas_call(kernel, out_shape=jax.ShapeDtypeStruct(leaf_out.shape, F32...  61.9 us
    unnamed x1, local copies, waits for them, and re-layouts  1.89 us

profile of v2, /device:TPU:1, one launch (start us, length us, event | category | flops | bytes accessed | tf_op | source)
XLA Modules:
  0.0 63.8 jit_solution(9710253229031543538)
XLA Ops:
  0.0 61.9 %far_field.1 = f32[2,64,1024]{2,1,0:T(8,128)} custom-call(bf16[2,64,1024]{2,1,0:T(8,128)(2,1)} %leaf_ref.1, bf16[1024,4096]{1,0:T(8,128)(2,1)} %matrix_ref.1, f32[8,4096]{1,0:T(8,128)} %shift_mid_ref.1, f32[632,128]{1,0:T(8,128)} %bitcast.14, f32[1264,128]{1,0:T(8,128)} %bitcast.12, bf16[256,1024]{1,0:T(8,128)(2,1)} %bitcast.13, f32[64,128]{1,0:T(8,128)} %bitcast.17, ...), custom_call_target="tpu_custom_call" | custom-call | tf_op jit(solution)/shard_map/far_field/pallas_call | solution.py:687
  61.9 1.9 %copy.14 = f32[2,64,1024]{2,1,0:T(8,128)} copy(f32[2,64,1024]{2,1,0:T(8,128)} %far_field.1) | data formatting | bytes 1048576

commit v3 on v2

--- a/solution.py
+++ b/solution.py
@@ -13,6 +13,7 @@
 PLANES = 4
 SECTORS = 16
 LANES = 128
+EARLY = 3
 
 
 def place():
@@ -129,6 +130,8 @@
     shift_top,
     lists_mid,
     lists_top,
+    scaled_mid,
+    scaled_top,
     list_s,
     offset_s,
     list_ts,
@@ -253,8 +256,6 @@
     piece[0:used, :] = trans_top[...].astype(BF16)
     piece[used:, :] = jnp.zeros((piece.shape[0] - used, LANES), BF16)
 
-    pl.semaphore_wait(barrier, SECTORS - 1 + 3 + (low + core) % 2)
-
     swap_copy = pltpu.make_async_remote_copy(
         src_ref=piece,
         dst_ref=t_all.at[z, low],
@@ -277,17 +278,6 @@
 
     def local_copy(index):
         return pltpu.make_async_copy(shared[index][0], shared[index][1], share_recv.at[index])
-
-    @pl.when(own)
-    def _():
-        for index in range(3):
-            share_copy(index).start()
-            local_copy(index).start()
-        t_all[z, core] = piece[...]
-
-    @pl.when(jnp.logical_not(own))
-    def _():
-        swap_copy.start()
 
     loads[2].wait()
     sines, cosines = sin_cos(shift_mid[...])
@@ -326,38 +316,63 @@
             device_id_type=MESH,
         )
 
-    def send_pair(k, carry):
+    def make_pair(k, carry):
         first, second = nth(2 * k), nth(2 * k + 1)
         sending[first] = parents(first, 0)
         sending[second] = parents(second, 1)
-        a2a_copy(first, sector).start()
-        a2a_copy(second, sector).start()
-        return carry
-
-    lax.fori_loop(0, 3, send_pair, 0)
+        return carry
+
+    def start_pair(k, carry):
+        a2a_copy(nth(2 * k), sector).start()
+        a2a_copy(nth(2 * k + 1), sector).start()
+        return carry
+
+    def send_pair(k, carry):
+        make_pair(k, carry)
+        return start_pair(k, carry)
+
+    lax.fori_loop(0, EARLY, make_pair, 0)
+    pl.semaphore_wait(barrier, SECTORS - 1 + 3 + (low + core) % 2)
+
+    @pl.when(own)
+    def _():
+        for index in range(3):
+            share_copy(index).start()
+            local_copy(index).start()
+        t_all[z, core] = piece[...]
 
     @pl.when(jnp.logical_not(own))
     def _():
-        swap_copy.wait()
-
-    t_spread.start_own()
-    lax.fori_loop(3, 7, send_pair, 0)
+        swap_copy.start()
+
+    lax.fori_loop(0, EARLY, start_pair, 0)
+    lax.fori_loop(EARLY, 7, send_pair, 0)
     last = nth(SECTORS - 2)
     sending[last] = parents(last, 0)
     a2a_copy(last, sector).start()
     p_all[z, core, pl.ds(pl.multiple_of(sector * 32, 32), 32), :] = parents(sector, 1)
-    t_spread.forward()
+
+    @pl.when(jnp.logical_not(own))
+    def _():
+        swap_copy.wait()
+
+    t_spread.start_own()
 
     for copy in loads[3:]:
         copy.wait()
+    scaled_mid[...] = lists_mid[...] * 8
+    scaled_top[0] = lists_top[0] * 16
+    scaled_top[1] = lists_top[1] * 8
     to_smem = [
         pltpu.make_async_copy(source, target, index_sem.at[index])
         for index, (source, target) in enumerate(
             (
-                (lists_mid.at[0], list_s),
-                (lists_mid.at[1], offset_s),
-                (lists_top.at[0], list_ts),
-                (lists_top.at[1], offset_ts),
+                (scaled_mid.at[0, :, 0:128], list_s.at[0]),
+                (scaled_mid.at[0, :, 128:256], list_s.at[1]),
+                (scaled_mid.at[1, :, 0:128], offset_s.at[0]),
+                (scaled_mid.at[1, :, 128:256], offset_s.at[1]),
+                (scaled_top.at[0], list_ts),
+                (scaled_top.at[1], offset_ts),
             )
         )
     ]
@@ -375,13 +390,12 @@
             share_copy(index).wait_recv()
 
     offsets = trans_mid.shape[0] // 4
-    t_rows = t_tab.reshape(offsets * 8, LANES)
 
     def put_offsets(first, row):
         for quarter, places in enumerate(((0, 2), (4, 6), (1, 3), (5, 7))):
             v = trans_mid[pl.ds(first + quarter, 8, stride=4), :]
             for at in places:
-                t_rows[pl.ds(row + at, 8, stride=8), :] = v
+                t_tab[pl.ds(row + at, 8, stride=8), :] = v
 
     def mid_offsets(k, carry):
         put_offsets(pl.multiple_of(k * 32, 32), pl.multiple_of(k * 64, 64))
@@ -444,13 +458,14 @@
     def mid_table(plane, side):
         def one(s, carry):
             odd = s % 2
-            first = (2 * plane + odd) * 128 + (s - odd + side) * 8
+            first = ((2 * plane + odd) * 128 + (s - odd + side) * 8) * 8
             found = p_all[plane, side, pl.ds(pl.multiple_of(s * 32, 32), 32), :].astype(F32)
             for pair in range(4):
                 v = found[pair * 8 : pair * 8 + 8]
                 r = pltpu.roll(v, 4, 0)
-                p_tab[first + pair * 2] = jnp.where(upper, v, r)
-                p_tab[first + pair * 2 + 1] = jnp.where(upper, r, v)
+                at = first + pair * 16
+                p_tab[pl.ds(pl.multiple_of(at, 8), 8), :] = jnp.where(upper, v, r)
+                p_tab[pl.ds(pl.multiple_of(at + 8, 8), 8), :] = jnp.where(upper, r, v)
             return carry
 
         lax.fori_loop(0, SECTORS, one, 0)
@@ -459,69 +474,51 @@
         def one(s, carry):
             odd = s % 2
             found = tp_all[plane, side, pl.ds(pl.multiple_of(s * 16, 16), 16), :].astype(F32)
-            first = (2 * plane + odd) * 16 + (s - odd + side)
-            p_top[first, 0] = found[:8]
-            p_top[first, 1] = found[8:]
+            first = ((2 * plane + odd) * 16 + (s - odd + side)) * 16
+            p_top[pl.ds(pl.multiple_of(first, 16), 16), :] = found
             return carry
 
         lax.fori_loop(0, SECTORS, one, 0)
 
     def offset_table(plane, side):
         at = plane * 2 + side
-        t_rows = t_top.reshape(t_top.shape[0] * 8, LANES)
 
         def one(k, carry):
             found = t_all[plane, side, pl.ds(pl.multiple_of(k * 16, 16), 16), :].astype(F32)
             for half in range(2):
-                t_rows[pl.ds(k * 128 + half * 64 + at, 8, stride=8), :] = found[half * 8 : half * 8 + 8]
+                t_top[pl.ds(k * 128 + half * 64 + at, 8, stride=8), :] = found[half * 8 : half * 8 + 8]
             return carry
 
         lax.fori_loop(0, t_all.shape[2] // 16, one, 0)
 
     mid_table(z, core)
     top_table(z, core)
-    t_spread.forward_far()
     offset_table(z, core)
-    offset_table(t_spread.left, core)
-    offset_table(t_spread.right, core)
+    t_spread.forward()
     p_spread.forward()
     tp_spread.forward()
     mid_table(p_spread.left, core)
     mid_table(p_spread.right, core)
-    offset_table(t_spread.far, core)
-    for which in range(3):
-        mid_table(p_spread.take(which), 1 - core)
+    mid_table(p_spread.take(0), 1 - core)
     p_spread.forward_far()
+    t_spread.forward_far()
     tp_spread.forward_far()
+    for plane in (p_spread.left, p_spread.right, p_spread.far):
+        offset_table(plane, core)
+        top_table(plane, core)
+    mid_table(p_spread.take(1), 1 - core)
+    mid_table(p_spread.take(2), 1 - core)
     mid_table(p_spread.far, core)
+    mid_table(p_spread.take(3), 1 - core)
     for which in range(4):
         offset_table(t_spread.take(which), 1 - core)
-    mid_table(p_spread.take(3), 1 - core)
+        top_table(tp_spread.take(which), 1 - core)
     for copy in to_smem:
         copy.wait()
 
     entries = list_mid_ref.shape[0]
 
-    def mid_box(k, carry):
-        s = k // 8
-        odd = s % 2
-        column = odd * 128 + (s - odd + core) * 8 + k % 8
-        kept = jnp.zeros((8, LANES), F32)
-        for j in range(entries):
-            p = p_tab[list_s[j, column]]
-            t = t_tab[offset_s[j, column]]
-            kept = kept + p * t
-        mid_sum[pl.ds(pl.multiple_of(k * 8, 8), 8), :] = kept
-        return carry
-
-    lax.fori_loop(0, SECTORS * 8, mid_box, 0)
-
-    for plane in (tp_spread.left, tp_spread.right, tp_spread.far):
-        top_table(plane, core)
-    for which in range(4):
-        top_table(tp_spread.take(which), 1 - core)
-
-    behind = trans_top_ref.shape[0] // 2
+    behind = (trans_top_ref.shape[0] // 2) * 8
 
     def top_box(k, carry):
         odd = k % 2
@@ -530,10 +527,10 @@
         for j in range(entries):
             n = list_ts[j, column]
             o = offset_ts[j, column]
-            pr = p_top[n, 0]
-            pi = p_top[n, 1]
-            tr = t_top[o]
-            ti = t_top[o + behind]
+            pr = p_top[pl.ds(n, 8), :]
+            pi = p_top[pl.ds(n + 8, 8), :]
+            tr = t_top[pl.ds(o, 8), :]
+            ti = t_top[pl.ds(o + behind, 8), :]
             sums = [sums[0] + pr * tr, sums[1] + pi * ti, sums[2] + pr * ti, sums[3] + pi * tr]
         real = (sums[0] - sums[1]).astype(BF16).astype(F32)
         imag = (sums[2] + sums[3]).astype(BF16).astype(F32)
@@ -577,11 +574,24 @@
         )
 
     def combine(k):
+        odd = k % 2
+        column = (k - odd + core) * 8
+
+        def mid_box(i, carry):
+            kept = jnp.zeros((8, LANES), F32)
+            for j in range(entries):
+                p = p_tab[pl.ds(list_s[odd, j, column + i], 8), :]
+                t = t_tab[pl.ds(offset_s[odd, j, column + i], 8), :]
+                kept = kept + p * t
+            mid_sum[pl.ds(pl.multiple_of(i * 8, 8), 8), :] = kept
+            return carry
+
+        lax.fori_loop(0, 8, mid_box, 0)
         at = pl.multiple_of(k * 8, 8)
         sides = []
         for side in range(2):
             lanes = slice(side * LANES, side * LANES + LANES)
-            parts = [mid_sum[pl.ds(k * 64 + side + 2 * quarter, 8, stride=8), :] for quarter in range(4)]
+            parts = [mid_sum[pl.ds(side + 2 * quarter, 8, stride=8), :] for quarter in range(4)]
             real = (parts[0] - parts[3]) + down[pl.ds(at, 8), lanes]
             imag = (parts[1] + parts[2]) + down[pl.ds(pl.multiple_of(128 + k * 8, 8), 8), lanes]
             sides.append(jnp.concatenate([real, imag], axis=0).astype(BF16))
@@ -699,8 +709,10 @@
             VMEM((64, LANES), F32),
             VMEM((2, entries, 256), jnp.int32),
             VMEM((2, entries, 128), jnp.int32),
-            pltpu.SMEM((entries, 256), jnp.int32),
-            pltpu.SMEM((entries, 256), jnp.int32),
+            VMEM((2, entries, 256), jnp.int32),
+            VMEM((2, entries, 128), jnp.int32),
+            pltpu.SMEM((2, entries, 128), jnp.int32),
+            pltpu.SMEM((2, entries, 128), jnp.int32),
             pltpu.SMEM((entries, 128), jnp.int32),
             pltpu.SMEM((entries, 128), jnp.int32),
             VMEM((PLANES, 2, 512, LANES), BF16),
@@ -717,11 +729,11 @@
             VMEM((256, LANES), F32),
             VMEM((64, LANES), F32),
             VMEM((64, LANES), F32),
-            VMEM((1024, 8, LANES), F32),
-            VMEM((offsets, 8, LANES), F32),
-            VMEM((128, 2, 8, LANES), F32),
-            VMEM((padded, 8, LANES), F32),
-            VMEM((128 * 8, LANES), F32),
+            VMEM((1024 * 8, LANES), F32),
+            VMEM((offsets * 8, LANES), F32),
+            VMEM((128 * 16, LANES), F32),
+            VMEM((padded * 8, LANES), F32),
+            VMEM((8 * 8, LANES), F32),
             VMEM((16 * 16, LANES), F32),
             VMEM((256, 1024), BF16),
             VMEM((256, 256), F32),
@@ -731,7 +743,7 @@
             VMEM((rows, interp_mid.shape[0]), F32),
             DMA((SECTORS,)),
             DMA((7,)),
-            DMA((4,)),
+            DMA((6,)),
             DMA((SECTORS,)),
             DMA((SECTORS,)),
             DMA((2,)),

time: 64.6 us -> 61.4 us (0.950); the launches traced: 63.8 us -> 61.2 us
  Pallas kernels: 61.9 us -> 59.3 us
    pallas_call x1, Pallas kernels: 61.9 us -> 59.3 us  [on_device(): pl.pallas_call(kernel, out_shape=jax.ShapeDtypeStruct(leaf_out.shape, F32...]
where the time goes in v3:
time: 61.4 us; the launch traced here: 61.2 us
  Pallas kernels  59.3 us (97%)
  local copies, waits for them, and re-layouts  1.89 us (3%)
    pallas_call x1, Pallas kernels, on_device(): pl.pallas_call(kernel, out_shape=jax.ShapeDtypeStruct(leaf_out.shape, F32...  59.3 us
    unnamed x1, local copies, waits for them, and re-layouts  1.89 us

profile of v3, /device:TPU:1, one launch (start us, length us, event | category | flops | bytes accessed | tf_op | source)
XLA Modules:
  0.0 61.2 jit_solution(15407584409769798680)
XLA Ops:
  0.0 59.3 %far_field.1 = f32[2,64,1024]{2,1,0:T(8,128)} custom-call(bf16[2,64,1024]{2,1,0:T(8,128)(2,1)} %leaf_ref.1, bf16[1024,4096]{1,0:T(8,128)(2,1)} %matrix_ref.1, f32[8,4096]{1,0:T(8,128)} %shift_mid_ref.1, f32[632,128]{1,0:T(8,128)} %bitcast.14, f32[1264,128]{1,0:T(8,128)} %bitcast.12, bf16[256,1024]{1,0:T(8,128)(2,1)} %bitcast.13, f32[64,128]{1,0:T(8,128)} %bitcast.17, ...), custom_call_target="tpu_custom_call" | custom-call | tf_op jit(solution)/shard_map/far_field/pallas_call | solution.py:697
  59.3 1.9 %copy.14 = f32[2,64,1024]{2,1,0:T(8,128)} copy(f32[2,64,1024]{2,1,0:T(8,128)} %far_field.1) | data formatting | bytes 1048576

commit v4 on v3

--- a/solution.py
+++ b/solution.py
@@ -13,7 +13,6 @@
 PLANES = 4
 SECTORS = 16
 LANES = 128
-EARLY = 3
 
 
 def place():
@@ -178,9 +177,9 @@
     tp_recv,
     back_send,
     back_recv,
-    out_sem,
 ):
     z, sector, core = place()
+    entries = list_mid_ref.shape[0]
     low = sector % 2
     own = low == core
     partner = device_of(z, sector, 1 - core)
@@ -191,8 +190,14 @@
     p_spread = Spread(p_all, p_send, p_recv)
     tp_spread = Spread(tp_all, tp_send, tp_recv)
 
+    group = sector // 4
+    inside = sector % 4
+
     def nth(k):
-        return (sector + 1 + k) % SECTORS
+        return ((group + 1 + k // 4) % 4) * 4 + (inside + 1 + k % 4) % 4
+
+    def from_nth(k):
+        return ((group + 7 - k // 4) % 4) * 4 + (inside + 7 - k % 4) % 4
 
     def to_sector(s):
         return device_of(z, s, core)
@@ -229,16 +234,12 @@
     for copy in loads[:3]:
         copy.start()
 
-    def weight_copy(s):
-        return pltpu.make_async_copy(
-            matrix_ref.at[:, pl.ds(pl.multiple_of(s * 256, 256), 256)], weights.at[s], weight_sem.at[s]
-        )
-
-    def start_weight(k, carry):
-        weight_copy(nth(k)).start()
-        return carry
-
-    lax.fori_loop(0, SECTORS, start_weight, 0)
+    def weight_copy(piece_at):
+        columns = pl.ds(pl.multiple_of((group + 1 + piece_at) % 4 * 1024, 1024), 1024)
+        return pltpu.make_async_copy(matrix_ref.at[:, columns], weights.at[:, columns], weight_sem.at[piece_at])
+
+    for piece_at in range(4):
+        weight_copy(piece_at).start()
     for copy in loads[3:]:
         copy.start()
 
@@ -286,8 +287,7 @@
 
     def parents(s, slot):
         columns = pl.ds(pl.multiple_of(s * 256, 256), 256)
-        weight_copy(s).wait()
-        spread = jnp.dot(leaf_rows[...], weights[s], preferred_element_type=F32)
+        spread = jnp.dot(leaf_rows[...], weights[:, columns], preferred_element_type=F32)
         real_sum = jnp.zeros((8, 256), F32)
         imag_sum = jnp.zeros((8, 256), F32)
         for child in range(8):
@@ -316,22 +316,17 @@
             device_id_type=MESH,
         )
 
-    def make_pair(k, carry):
-        first, second = nth(2 * k), nth(2 * k + 1)
-        sending[first] = parents(first, 0)
-        sending[second] = parents(second, 1)
-        return carry
-
-    def start_pair(k, carry):
-        a2a_copy(nth(2 * k), sector).start()
-        a2a_copy(nth(2 * k + 1), sector).start()
-        return carry
-
-    def send_pair(k, carry):
-        make_pair(k, carry)
-        return start_pair(k, carry)
-
-    lax.fori_loop(0, EARLY, make_pair, 0)
+    def make_four(piece_at):
+        weight_copy(piece_at).wait()
+        for slot in range(4):
+            s = nth(piece_at * 4 + slot)
+            sending[s] = parents(s, slot)
+
+    def start_four(piece_at):
+        for slot in range(4):
+            a2a_copy(nth(piece_at * 4 + slot), sector).start()
+
+    make_four(0)
     pl.semaphore_wait(barrier, SECTORS - 1 + 3 + (low + core) % 2)
 
     @pl.when(own)
@@ -340,41 +335,46 @@
             share_copy(index).start()
             local_copy(index).start()
         t_all[z, core] = piece[...]
+        t_spread.start_own()
 
     @pl.when(jnp.logical_not(own))
     def _():
         swap_copy.start()
 
-    lax.fori_loop(0, EARLY, start_pair, 0)
-    lax.fori_loop(EARLY, 7, send_pair, 0)
-    last = nth(SECTORS - 2)
-    sending[last] = parents(last, 0)
-    a2a_copy(last, sector).start()
-    p_all[z, core, pl.ds(pl.multiple_of(sector * 32, 32), 32), :] = parents(sector, 1)
+    start_four(0)
+
+    def send_four(piece_at, carry):
+        make_four(piece_at)
+        start_four(piece_at)
+        return carry
+
+    lax.fori_loop(1, 3, send_four, 0)
+    weight_copy(3).wait()
+    for slot in range(3):
+        s = nth(12 + slot)
+        sending[s] = parents(s, slot)
+        a2a_copy(s, sector).start()
+    p_all[z, core, pl.ds(pl.multiple_of(sector * 32, 32), 32), :] = parents(sector, 3)
 
     @pl.when(jnp.logical_not(own))
     def _():
         swap_copy.wait()
-
-    t_spread.start_own()
+        t_spread.start_own()
+
 
     for copy in loads[3:]:
         copy.wait()
-    scaled_mid[...] = lists_mid[...] * 8
-    scaled_top[0] = lists_top[0] * 16
-    scaled_top[1] = lists_top[1] * 8
+    scaled = jnp.transpose(jnp.concatenate([lists_mid[0], lists_mid[1]], axis=0) * 8)
+    scaled_mid[0] = scaled[:, :entries]
+    scaled_mid[1] = scaled[:, entries:]
+    scaled = jnp.transpose(jnp.concatenate([lists_top[0] * 16, lists_top[1] * 8], axis=0))
+    scaled_top[0] = scaled[:, :entries]
+    scaled_top[1] = scaled[:, entries:]
     to_smem = [
-        pltpu.make_async_copy(source, target, index_sem.at[index])
-        for index, (source, target) in enumerate(
-            (
-                (scaled_mid.at[0, :, 0:128], list_s.at[0]),
-                (scaled_mid.at[0, :, 128:256], list_s.at[1]),
-                (scaled_mid.at[1, :, 0:128], offset_s.at[0]),
-                (scaled_mid.at[1, :, 128:256], offset_s.at[1]),
-                (scaled_top.at[0], list_ts),
-                (scaled_top.at[1], offset_ts),
-            )
-        )
+        pltpu.make_async_copy(scaled_mid.at[0], list_s, index_sem.at[0]),
+        pltpu.make_async_copy(scaled_mid.at[1], offset_s, index_sem.at[1]),
+        pltpu.make_async_copy(scaled_top.at[0], list_ts, index_sem.at[2]),
+        pltpu.make_async_copy(scaled_top.at[1], offset_ts, index_sem.at[3]),
     ]
     for copy in to_smem:
         copy.start()
@@ -456,67 +456,76 @@
     upper = lax.broadcasted_iota(jnp.int32, (8, LANES), 0) < 4
 
     def mid_table(plane, side):
-        def one(s, carry):
-            odd = s % 2
-            first = ((2 * plane + odd) * 128 + (s - odd + side) * 8) * 8
-            found = p_all[plane, side, pl.ds(pl.multiple_of(s * 32, 32), 32), :].astype(F32)
-            for pair in range(4):
-                v = found[pair * 8 : pair * 8 + 8]
-                r = pltpu.roll(v, 4, 0)
-                at = first + pair * 16
-                p_tab[pl.ds(pl.multiple_of(at, 8), 8), :] = jnp.where(upper, v, r)
-                p_tab[pl.ds(pl.multiple_of(at + 8, 8), 8), :] = jnp.where(upper, r, v)
+        def four(k, carry):
+            for part in range(4):
+                odd = part % 2
+                found = p_all[plane, side, pl.ds(pl.multiple_of(k * 128 + part * 32, 32), 32), :].astype(F32)
+                first = ((2 * plane + odd) * 128 + (k * 4 + part - odd + side) * 8) * 8
+                for pair in range(4):
+                    v = found[pair * 8 : pair * 8 + 8]
+                    r = pltpu.roll(v, 4, 0)
+                    at = first + pair * 16
+                    p_tab[pl.ds(pl.multiple_of(at, 8), 8), :] = jnp.where(upper, v, r)
+                    p_tab[pl.ds(pl.multiple_of(at + 8, 8), 8), :] = jnp.where(upper, r, v)
             return carry
 
-        lax.fori_loop(0, SECTORS, one, 0)
+        lax.fori_loop(0, SECTORS // 4, four, 0)
 
     def top_table(plane, side):
-        def one(s, carry):
-            odd = s % 2
-            found = tp_all[plane, side, pl.ds(pl.multiple_of(s * 16, 16), 16), :].astype(F32)
-            first = ((2 * plane + odd) * 16 + (s - odd + side)) * 16
-            p_top[pl.ds(pl.multiple_of(first, 16), 16), :] = found
+        def four(k, carry):
+            for part in range(4):
+                odd = part % 2
+                found = tp_all[plane, side, pl.ds(pl.multiple_of(k * 64 + part * 16, 16), 16), :].astype(F32)
+                first = ((2 * plane + odd) * 16 + (k * 4 + part - odd + side)) * 16
+                p_top[pl.ds(pl.multiple_of(first, 16), 16), :] = found
             return carry
 
-        lax.fori_loop(0, SECTORS, one, 0)
+        lax.fori_loop(0, SECTORS // 4, four, 0)
 
     def offset_table(plane, side):
         at = plane * 2 + side
 
-        def one(k, carry):
-            found = t_all[plane, side, pl.ds(pl.multiple_of(k * 16, 16), 16), :].astype(F32)
-            for half in range(2):
-                t_top[pl.ds(k * 128 + half * 64 + at, 8, stride=8), :] = found[half * 8 : half * 8 + 8]
+        def four(k, carry):
+            for part in range(4):
+                found = t_all[plane, side, pl.ds(pl.multiple_of(k * 64 + part * 16, 16), 16), :].astype(F32)
+                for half in range(2):
+                    t_top[pl.ds(k * 512 + part * 128 + half * 64 + at, 8, stride=8), :] = found[
+                        half * 8 : half * 8 + 8
+                    ]
             return carry
 
-        lax.fori_loop(0, t_all.shape[2] // 16, one, 0)
+        lax.fori_loop(0, t_all.shape[2] // 64, four, 0)
 
     mid_table(z, core)
     top_table(z, core)
     offset_table(z, core)
     t_spread.forward()
+    offset_table(t_spread.left, core)
+    offset_table(t_spread.right, core)
     p_spread.forward()
     tp_spread.forward()
     mid_table(p_spread.left, core)
     mid_table(p_spread.right, core)
+    t_spread.forward_far()
+    offset_table(t_spread.far, core)
+    offset_table(t_spread.take(0), 1 - core)
     mid_table(p_spread.take(0), 1 - core)
+    top_table(tp_spread.left, core)
+    top_table(tp_spread.right, core)
     p_spread.forward_far()
-    t_spread.forward_far()
     tp_spread.forward_far()
-    for plane in (p_spread.left, p_spread.right, p_spread.far):
-        offset_table(plane, core)
-        top_table(plane, core)
+    mid_table(p_spread.far, core)
+    top_table(tp_spread.far, core)
     mid_table(p_spread.take(1), 1 - core)
     mid_table(p_spread.take(2), 1 - core)
-    mid_table(p_spread.far, core)
+    for which in range(1, 4):
+        offset_table(t_spread.take(which), 1 - core)
+    for which in range(4):
+        top_table(tp_spread.take(which), 1 - core)
     mid_table(p_spread.take(3), 1 - core)
-    for which in range(4):
-        offset_table(t_spread.take(which), 1 - core)
-        top_table(tp_spread.take(which), 1 - core)
     for copy in to_smem:
         copy.wait()
 
-    entries = list_mid_ref.shape[0]
 
     behind = (trans_top_ref.shape[0] // 2) * 8
 
@@ -525,8 +534,8 @@
         column = (2 * z + odd) * 16 + (k - odd + core)
         sums = [jnp.zeros((8, LANES), F32) for _ in range(4)]
         for j in range(entries):
-            n = list_ts[j, column]
-            o = offset_ts[j, column]
+            n = list_ts[column, j]
+            o = offset_ts[column, j]
             pr = p_top[pl.ds(n, 8), :]
             pi = p_top[pl.ds(n + 8, 8), :]
             tr = t_top[pl.ds(o, 8), :]
@@ -575,13 +584,13 @@
 
     def combine(k):
         odd = k % 2
-        column = (k - odd + core) * 8
+        first = odd * 128 + (k - odd + core) * 8
 
         def mid_box(i, carry):
             kept = jnp.zeros((8, LANES), F32)
             for j in range(entries):
-                p = p_tab[pl.ds(list_s[odd, j, column + i], 8), :]
-                t = t_tab[pl.ds(offset_s[odd, j, column + i], 8), :]
+                p = p_tab[pl.ds(list_s[first + i, j], 8), :]
+                t = t_tab[pl.ds(offset_s[first + i, j], 8), :]
                 kept = kept + p * t
             mid_sum[pl.ds(pl.multiple_of(i * 8, 8), 8), :] = kept
             return carry
@@ -596,16 +605,6 @@
             imag = (parts[1] + parts[2]) + down[pl.ds(pl.multiple_of(128 + k * 8, 8), 8), lanes]
             sides.append(jnp.concatenate([real, imag], axis=0).astype(BF16))
         return jnp.concatenate(sides, axis=1)
-
-    def send_back(k, carry):
-        s = nth(k)
-        pieces[s] = combine(s)
-        back_copy(s, sector).start()
-        return carry
-
-    lax.fori_loop(0, SECTORS - 1, send_back, 0)
-    received[sector] = combine(sector)
-    total[...] = jnp.zeros_like(total)
 
     def finish_sector(s):
         columns = pl.ds(pl.multiple_of(s * 256, 256), 256)
@@ -624,26 +623,36 @@
             children[pair * 16 : pair * 16 + 16, :] = jnp.concatenate(reals, axis=0).astype(BF16)
             children[64 + pair * 16 : 80 + pair * 16, :] = jnp.concatenate(imags, axis=0).astype(BF16)
         total[...] += lax.dot_general(
-            children[...], weights[s], (((1,), (1,)), ((), ())), preferred_element_type=F32
+            children[...], weights[:, columns], (((1,), (1,)), ((), ())), preferred_element_type=F32
         )
 
-    finish_sector(sector)
+    total[...] = jnp.zeros_like(total)
+    late = 3
+
+    def send_back(k, carry):
+        s = nth(k)
+        pieces[s] = combine(s)
+        back_copy(s, sector).start()
+        return carry
 
     def take_back(k, carry):
-        s = nth(k)
+        s = from_nth(k)
         back_copy(s, s).wait_recv()
         finish_sector(s)
         return carry
 
-    lax.fori_loop(0, SECTORS - 1, take_back, 0)
-    total[...] = total[...] * (matrix_ref.shape[0] / matrix_ref.shape[1])
+    def send_and_take(k, carry):
+        send_back(k, carry)
+        return take_back(k - late, carry)
+
+    lax.fori_loop(0, late, send_back, 0)
+    lax.fori_loop(late, SECTORS - 1, send_and_take, 0)
+    received[sector] = combine(sector)
+    finish_sector(sector)
+    lax.fori_loop(SECTORS - 1 - late, SECTORS - 1, take_back, 0)
     half_rows = total.shape[0] // 2
-    outs = [
-        pltpu.make_async_copy(total.at[pl.ds(part * half_rows, half_rows)], out_ref.at[part], out_sem.at[part])
-        for part in range(2)
-    ]
-    for copy in outs:
-        copy.start()
+    for part in range(2):
+        out_ref[part] = total[part * half_rows : part * half_rows + half_rows, :]
 
     def wait_sent(k, carry):
         s = nth(k)
@@ -660,8 +669,6 @@
 
     for each in (t_spread, p_spread, tp_spread):
         each.sent()
-    for copy in outs:
-        copy.wait()
 
 
 def on_device(
@@ -694,14 +701,14 @@
         offset_top.T,
     )
     padded = 640
-    return pl.pallas_call(
+    result = pl.pallas_call(
         kernel,
         out_shape=jax.ShapeDtypeStruct(leaf_out.shape, F32),
         in_specs=[pl.BlockSpec(memory_space=pltpu.HBM)] * len(operands),
-        out_specs=pl.BlockSpec(memory_space=pltpu.HBM),
+        out_specs=pl.BlockSpec(memory_space=VMEM),
         scratch_shapes=[
             VMEM(leaf_out.shape, BF16),
-            VMEM((SECTORS, interp_mid.shape[0], 256), BF16),
+            VMEM(interp_mid.shape, BF16),
             VMEM(shift_mid.shape, F32),
             VMEM((2 * offsets, LANES), F32),
             VMEM((4 * offsets, LANES), F32),
@@ -709,12 +716,12 @@
             VMEM((64, LANES), F32),
             VMEM((2, entries, 256), jnp.int32),
             VMEM((2, entries, 128), jnp.int32),
-            VMEM((2, entries, 256), jnp.int32),
-            VMEM((2, entries, 128), jnp.int32),
-            pltpu.SMEM((2, entries, 128), jnp.int32),
-            pltpu.SMEM((2, entries, 128), jnp.int32),
-            pltpu.SMEM((entries, 128), jnp.int32),
-            pltpu.SMEM((entries, 128), jnp.int32),
+            VMEM((2, 256, entries), jnp.int32),
+            VMEM((2, 128, entries), jnp.int32),
+            pltpu.SMEM((256, entries), jnp.int32),
+            pltpu.SMEM((256, entries), jnp.int32),
+            pltpu.SMEM((128, entries), jnp.int32),
+            pltpu.SMEM((128, entries), jnp.int32),
             VMEM((PLANES, 2, 512, LANES), BF16),
             VMEM((PLANES, 2, 256, LANES), BF16),
             VMEM((PLANES, 2, padded, LANES), BF16),
@@ -722,7 +729,7 @@
             VMEM(shift_mid.shape, F32),
             VMEM(shift_mid.shape, F32),
             VMEM((SECTORS, 32, LANES), BF16),
-            VMEM((64, LANES), F32),
+            VMEM((128, LANES), F32),
             VMEM((padded, LANES), BF16),
             VMEM((512, LANES), F32),
             VMEM((256, 256), BF16),
@@ -741,9 +748,9 @@
             VMEM((SECTORS, 16, 256), BF16),
             VMEM((rows, 256), BF16),
             VMEM((rows, interp_mid.shape[0]), F32),
-            DMA((SECTORS,)),
+            DMA((4,)),
             DMA((7,)),
-            DMA((6,)),
+            DMA((4,)),
             DMA((SECTORS,)),
             DMA((SECTORS,)),
             DMA((2,)),
@@ -757,13 +764,13 @@
             DMA((8,)),
             DMA((SECTORS,)),
             DMA((SECTORS,)),
-            DMA((2,)),
         ],
         compiler_params=pltpu.CompilerParams(
             collective_id=0, has_side_effects=True, vmem_limit_bytes=60 * 1024 * 1024
         ),
         name="far_field",
     )(*operands)
+    return result * (interp_mid.shape[0] / interp_mid.shape[1])
 
 
 def solution(mesh):

time: 61.4 us -> 53.8 us (0.88)
  the two profiles are of different devices: /device:TPU:1 before, /device:TPU:12 now
where the time goes in v4:
time: 53.8 us; the launch traced here: 53.7 us
  Pallas kernels  51.8 us (96%)
  other arithmetic  1.88 us (3%)
    pallas_call x1, Pallas kernels, on_device(): pl.pallas_call(kernel, out_shape=jax.ShapeDtypeStruct(leaf_out.shape, F32...  51.8 us
    mul x1, other arithmetic, on_device(): return result * (interp_mid.shape[0] / interp_mid.shape[1])  1.88 us

profile of v4, /device:TPU:12, one launch (start us, length us, event | category | flops | bytes accessed | tf_op | source)
XLA Modules:
  0.0 53.7 jit_solution(3182595577657209596)
XLA Ops:
  0.0 51.8 %far_field.1 = f32[2,64,1024]{2,1,0:T(8,128)} custom-call(bf16[2,64,1024]{2,1,0:T(8,128)(2,1)} %leaf_ref.1, bf16[1024,4096]{1,0:T(8,128)(2,1)} %matrix_ref.1, f32[8,4096]{1,0:T(8,128)} %shift_mid_ref.1, f32[632,128]{1,0:T(8,128)} %bitcast.14, f32[1264,128]{1,0:T(8,128)} %bitcast.12, bf16[256,1024]{1,0:T(8,128)(2,1)} %bitcast.13, f32[64,128]{1,0:T(8,128)} %bitcast.17, ...), custom_call_target="tpu_custom_call" | custom-call | tf_op jit(solution)/shard_map/far_field/pallas_call | solution.py:704
  51.8 1.9 %broadcast_multiply_fusion = f32[2,64,1024]{2,1,0:T(8,128)} fusion(f32[2,64,1024]{2,1,0:T(8,128)} %far_field.1), kind=kLoop, calls=%fused_computation | loop fusion | flops 131072 | bytes 1048576 | tf_op jit(solution)/shard_map/mul | solution.py:773

commit v5 on v4

--- a/solution.py
+++ b/solution.py
@@ -76,16 +76,22 @@
         )
 
     def start_own(self):
-        self.copy(self.z, self.core, None, 0, self.to_right).start()
-        self.copy(self.z, self.core, None, 1, self.to_left).start()
+        self.copy(self.z, self.core, 0, 0, self.to_right).start()
+        self.copy(self.z, self.core, 1, 1, self.to_left).start()
+        self.copy(self.z, self.core, 1, 8, self.to_right).start()
+        self.copy(self.z, self.core, 0, 9, self.to_left).start()
         self.copy(self.z, self.core, None, 4, self.partner).start()
 
     def forward(self):
-        self.copy(self.left, self.core, None, 0, self.to_right).wait_recv()
+        self.copy(self.left, self.core, 0, 0, self.to_right).wait_recv()
         self.copy(self.left, self.core, 0, 2, self.to_right).start()
+        self.copy(self.right, self.core, 1, 1, self.to_left).wait_recv()
+        self.copy(self.right, self.core, 1, 3, self.to_left).start()
+
+    def forward_rest(self):
+        self.copy(self.left, self.core, 1, 8, self.to_right).wait_recv()
         self.copy(self.left, self.core, None, 5, self.partner).start()
-        self.copy(self.right, self.core, None, 1, self.to_left).wait_recv()
-        self.copy(self.right, self.core, 1, 3, self.to_left).start()
+        self.copy(self.right, self.core, 0, 9, self.to_left).wait_recv()
         self.copy(self.right, self.core, None, 6, self.partner).start()
 
     def forward_far(self):
@@ -99,8 +105,10 @@
         return plane
 
     def sent(self):
-        self.copy(self.z, self.core, None, 0, self.to_right).wait_send()
-        self.copy(self.z, self.core, None, 1, self.to_left).wait_send()
+        self.copy(self.z, self.core, 0, 0, self.to_right).wait_send()
+        self.copy(self.z, self.core, 1, 1, self.to_left).wait_send()
+        self.copy(self.z, self.core, 1, 8, self.to_right).wait_send()
+        self.copy(self.z, self.core, 0, 9, self.to_left).wait_send()
         self.copy(self.left, self.core, 0, 2, self.to_right).wait_send()
         self.copy(self.right, self.core, 1, 3, self.to_left).wait_send()
         for index, plane in self.crossing:
@@ -193,11 +201,15 @@
     group = sector // 4
     inside = sector % 4
 
+    def apart(a, k):
+        high = (a // 2 + k + 1) % 2
+        return high * 2 + (a % 2 + 1 + k // 2) % 2
+
     def nth(k):
-        return ((group + 1 + k // 4) % 4) * 4 + (inside + 1 + k % 4) % 4
-
-    def from_nth(k):
-        return ((group + 7 - k // 4) % 4) * 4 + (inside + 7 - k % 4) % 4
+        return apart(group, k // 4) * 4 + apart(inside, k % 4)
+
+    def other(k):
+        return (sector + 1 + k) % SECTORS
 
     def to_sector(s):
         return device_of(z, s, core)
@@ -205,7 +217,7 @@
     barrier = pltpu.get_barrier_semaphore()
 
     def signal_peer(k, carry):
-        pl.semaphore_signal(barrier, inc=1, device_id=to_sector(nth(k)), device_id_type=MESH)
+        pl.semaphore_signal(barrier, inc=1, device_id=to_sector(other(k)), device_id_type=MESH)
         return carry
 
     lax.fori_loop(0, SECTORS - 1, signal_peer, 0)
@@ -235,7 +247,7 @@
         copy.start()
 
     def weight_copy(piece_at):
-        columns = pl.ds(pl.multiple_of((group + 1 + piece_at) % 4 * 1024, 1024), 1024)
+        columns = pl.ds(pl.multiple_of(apart(group, piece_at) * 1024, 1024), 1024)
         return pltpu.make_async_copy(matrix_ref.at[:, columns], weights.at[:, columns], weight_sem.at[piece_at])
 
     for piece_at in range(4):
@@ -356,11 +368,6 @@
         a2a_copy(s, sector).start()
     p_all[z, core, pl.ds(pl.multiple_of(sector * 32, 32), 32), :] = parents(sector, 3)
 
-    @pl.when(jnp.logical_not(own))
-    def _():
-        swap_copy.wait()
-        t_spread.start_own()
-
 
     for copy in loads[3:]:
         copy.wait()
@@ -410,7 +417,7 @@
     sin_top[...] = sines_t
 
     def wait_sector(k, carry):
-        s = nth(k)
+        s = other(k)
         a2a_copy(s, s).wait_recv()
         return carry
 
@@ -451,7 +458,6 @@
 
     lax.fori_loop(0, 4, top_columns, 0)
     tp_all[z, core] = top_f32[...].astype(BF16)
-    tp_spread.start_own()
 
     upper = lax.broadcasted_iota(jnp.int32, (8, LANES), 0) < 4
 
@@ -498,34 +504,62 @@
 
     mid_table(z, core)
     top_table(z, core)
-    offset_table(z, core)
-    t_spread.forward()
-    offset_table(t_spread.left, core)
-    offset_table(t_spread.right, core)
     p_spread.forward()
-    tp_spread.forward()
+    tp_spread.start_own()
+    p_spread.forward_rest()
+
+    @pl.when(jnp.logical_not(own))
+    def _():
+        swap_copy.wait()
+        t_spread.start_own()
+
     mid_table(p_spread.left, core)
     mid_table(p_spread.right, core)
-    t_spread.forward_far()
-    offset_table(t_spread.far, core)
-    offset_table(t_spread.take(0), 1 - core)
     mid_table(p_spread.take(0), 1 - core)
-    top_table(tp_spread.left, core)
-    top_table(tp_spread.right, core)
+    for copy in to_smem:
+        copy.wait()
     p_spread.forward_far()
-    tp_spread.forward_far()
     mid_table(p_spread.far, core)
-    top_table(tp_spread.far, core)
     mid_table(p_spread.take(1), 1 - core)
     mid_table(p_spread.take(2), 1 - core)
-    for which in range(1, 4):
+    mid_table(p_spread.take(3), 1 - core)
+
+    def middle(k):
+        s = nth(k)
+        odd = s % 2
+        first = odd * 128 + (s - odd + core) * 8
+
+        def mid_box(i, carry):
+            kept = jnp.zeros((8, LANES), F32)
+            for j in range(entries):
+                p = p_tab[pl.ds(list_s[first + i, j], 8), :]
+                t = t_tab[pl.ds(offset_s[first + i, j], 8), :]
+                kept = kept + p * t
+            mid_sum[pl.ds(pl.multiple_of(k * 64 + i * 8, 8), 8), :] = kept
+            return carry
+
+        lax.fori_loop(0, 8, mid_box, 0)
+
+    def middle_early(k, carry):
+        middle(k)
+        return carry
+
+    ahead = 8
+    lax.fori_loop(0, 4, middle_early, 0)
+    tp_spread.forward()
+    t_spread.forward()
+    tp_spread.forward_rest()
+    t_spread.forward_rest()
+    lax.fori_loop(4, ahead, middle_early, 0)
+    tp_spread.forward_far()
+    t_spread.forward_far()
+    for plane in (z, t_spread.left, t_spread.right, t_spread.far):
+        offset_table(plane, core)
+    for plane in (tp_spread.left, tp_spread.right, tp_spread.far):
+        top_table(plane, core)
+    for which in range(4):
         offset_table(t_spread.take(which), 1 - core)
-    for which in range(4):
         top_table(tp_spread.take(which), 1 - core)
-    mid_table(p_spread.take(3), 1 - core)
-    for copy in to_smem:
-        copy.wait()
-
 
     behind = (trans_top_ref.shape[0] // 2) * 8
 
@@ -582,35 +616,24 @@
             device_id_type=MESH,
         )
 
-    def combine(k):
-        odd = k % 2
-        first = odd * 128 + (k - odd + core) * 8
-
-        def mid_box(i, carry):
-            kept = jnp.zeros((8, LANES), F32)
-            for j in range(entries):
-                p = p_tab[pl.ds(list_s[first + i, j], 8), :]
-                t = t_tab[pl.ds(offset_s[first + i, j], 8), :]
-                kept = kept + p * t
-            mid_sum[pl.ds(pl.multiple_of(i * 8, 8), 8), :] = kept
-            return carry
-
-        lax.fori_loop(0, 8, mid_box, 0)
+    def combine(n):
+        k = nth(n)
         at = pl.multiple_of(k * 8, 8)
         sides = []
         for side in range(2):
             lanes = slice(side * LANES, side * LANES + LANES)
-            parts = [mid_sum[pl.ds(side + 2 * quarter, 8, stride=8), :] for quarter in range(4)]
+            parts = [mid_sum[pl.ds(n * 64 + side + 2 * quarter, 8, stride=8), :] for quarter in range(4)]
             real = (parts[0] - parts[3]) + down[pl.ds(at, 8), lanes]
             imag = (parts[1] + parts[2]) + down[pl.ds(pl.multiple_of(128 + k * 8, 8), 8), lanes]
             sides.append(jnp.concatenate([real, imag], axis=0).astype(BF16))
         return jnp.concatenate(sides, axis=1)
 
-    def finish_sector(s):
+    def make_children(s, at):
         columns = pl.ds(pl.multiple_of(s * 256, 256), 256)
         c = cos_mid[:, columns]
         n = sin_mid[:, columns]
         found = received[s].astype(F32)
+        target = pl.ds(pl.multiple_of(at * 256, 256), 256)
         for pair in range(4):
             reals = []
             imags = []
@@ -620,42 +643,57 @@
                 imag = jnp.broadcast_to(found[8 + box : 9 + box], (8, 256))
                 reals.append(real * c + imag * n)
                 imags.append(imag * c - real * n)
-            children[pair * 16 : pair * 16 + 16, :] = jnp.concatenate(reals, axis=0).astype(BF16)
-            children[64 + pair * 16 : 80 + pair * 16, :] = jnp.concatenate(imags, axis=0).astype(BF16)
-        total[...] += lax.dot_general(
-            children[...], weights[:, columns], (((1,), (1,)), ((), ())), preferred_element_type=F32
-        )
-
-    total[...] = jnp.zeros_like(total)
-    late = 3
+            children[pair * 16 : pair * 16 + 16, target] = jnp.concatenate(reals, axis=0).astype(BF16)
+            children[64 + pair * 16 : 80 + pair * 16, target] = jnp.concatenate(imags, axis=0).astype(BF16)
+
+    def finish(piece_at, first, count):
+        at = apart(group, piece_at)
+        for slot in range(count):
+            back_copy(at * 4 + apart(inside, slot), at * 4 + apart(inside, slot)).wait_recv()
+        for slot in range(4):
+            make_children(at * 4 + slot, slot)
+        columns = pl.ds(pl.multiple_of(at * 1024, 1024), 1024)
+
+        def quarter(k, carry):
+            rows_at = pl.ds(pl.multiple_of(k * 256, 256), 256)
+            part = lax.dot_general(
+                weights[rows_at, columns], children[...], (((1,), (1,)), ((), ())), preferred_element_type=F32
+            )
+            if first:
+                total[rows_at, :] = part
+            else:
+                total[rows_at, :] += part
+            return carry
+
+        lax.fori_loop(0, 4, quarter, 0)
 
     def send_back(k, carry):
         s = nth(k)
-        pieces[s] = combine(s)
+        pieces[s] = combine(k)
         back_copy(s, sector).start()
         return carry
 
-    def take_back(k, carry):
-        s = from_nth(k)
-        back_copy(s, s).wait_recv()
-        finish_sector(s)
-        return carry
-
-    def send_and_take(k, carry):
-        send_back(k, carry)
-        return take_back(k - late, carry)
-
-    lax.fori_loop(0, late, send_back, 0)
-    lax.fori_loop(late, SECTORS - 1, send_and_take, 0)
-    received[sector] = combine(sector)
-    finish_sector(sector)
-    lax.fori_loop(SECTORS - 1 - late, SECTORS - 1, take_back, 0)
-    half_rows = total.shape[0] // 2
-    for part in range(2):
-        out_ref[part] = total[part * half_rows : part * half_rows + half_rows, :]
+    def middle_and_send(k, carry):
+        middle(k)
+        return send_back(k, carry)
+
+    lax.fori_loop(0, ahead, send_back, 0)
+    lax.fori_loop(ahead, SECTORS - 1, middle_and_send, 0)
+    middle(SECTORS - 1)
+    received[sector] = combine(SECTORS - 1)
+    finish(0, True, 4)
+    finish(1, False, 4)
+    finish(2, False, 4)
+    finish(3, False, 3)
+    half_rows = out_ref.shape[1]
+    for k in range(total.shape[0] // LANES):
+        columns = slice(k * LANES, k * LANES + LANES)
+        turned = jnp.transpose(total[columns, :])
+        for part in range(2):
+            out_ref[part, :, columns] = turned[part * half_rows : part * half_rows + half_rows]
 
     def wait_sent(k, carry):
-        s = nth(k)
+        s = other(k)
         a2a_copy(s, sector).wait_send()
         back_copy(s, sector).wait_send()
         return carry
@@ -703,7 +741,7 @@
     padded = 640
     result = pl.pallas_call(
         kernel,
-        out_shape=jax.ShapeDtypeStruct(leaf_out.shape, F32),
+        out_shape=VMEM(leaf_out.shape, F32),
         in_specs=[pl.BlockSpec(memory_space=pltpu.HBM)] * len(operands),
         out_specs=pl.BlockSpec(memory_space=VMEM),
         scratch_shapes=[
@@ -740,14 +778,14 @@
             VMEM((offsets * 8, LANES), F32),
             VMEM((128 * 16, LANES), F32),
             VMEM((padded * 8, LANES), F32),
-            VMEM((8 * 8, LANES), F32),
+            VMEM((128 * 8, LANES), F32),
             VMEM((16 * 16, LANES), F32),
             VMEM((256, 1024), BF16),
             VMEM((256, 256), F32),
             VMEM((SECTORS, 16, 256), BF16),
             VMEM((SECTORS, 16, 256), BF16),
-            VMEM((rows, 256), BF16),
-            VMEM((rows, interp_mid.shape[0]), F32),
+            VMEM((rows, 1024), BF16),
+            VMEM((interp_mid.shape[0], rows), F32),
             DMA((4,)),
             DMA((7,)),
             DMA((4,)),
@@ -756,12 +794,12 @@
             DMA((2,)),
             DMA((3,)),
             DMA((3,)),
-            DMA((8,)),
-            DMA((8,)),
-            DMA((8,)),
-            DMA((8,)),
-            DMA((8,)),
-            DMA((8,)),
+            DMA((10,)),
+            DMA((10,)),
+            DMA((10,)),
+            DMA((10,)),
+            DMA((10,)),
+            DMA((10,)),
             DMA((SECTORS,)),
             DMA((SECTORS,)),
         ],

time: 53.8 us -> 50 us (0.929)
  the two profiles are of different devices: /device:TPU:12 before, /device:TPU:1 now
where the time goes in v5:
time: 50 us; the launch traced here: 49.9 us
  Pallas kernels  49.1 us (98%)
  other arithmetic  0.84 us (2%)
    pallas_call x1, Pallas kernels, on_device(): pl.pallas_call(kernel, out_shape=VMEM(leaf_out.shape, F32), in_specs=[pl....  49.1 us

profile of v5, /device:TPU:1, one launch (start us, length us, event | category | flops | bytes accessed | tf_op | source)
XLA Modules:
  0.0 49.9 jit_solution(8495233581546138603)
XLA Ops:
  0.0 49.1 %far_field.1 = f32[2,64,1024]{2,1,0:T(8,128)S(1)} custom-call(bf16[2,64,1024]{2,1,0:T(8,128)(2,1)} %leaf_ref.1, bf16[1024,4096]{1,0:T(8,128)(2,1)} %matrix_ref.1, f32[8,4096]{1,0:T(8,128)} %shift_mid_ref.1, f32[632,128]{1,0:T(8,128)} %bitcast.14, f32[1264,128]{1,0:T(8,128)} %bitcast.12, bf16[256,1024]{1,0:T(8,128)(2,1)} %bitcast.13, f32[64,128]{1,0:T(8,128)} %bitcast.17, ...), custom_call_target="tpu_custom_call" | custom-call | tf_op jit(solution)/shard_map/far_field/pallas_call | solution.py:742
  49.1 0.8 %broadcast_multiply_fusion = f32[2,64,1024]{2,1,0:T(8,128)} fusion(f32[2,64,1024]{2,1,0:T(8,128)S(1)} %far_field.1), kind=kLoop, calls=%fused_computation | loop fusion | flops 131072 | bytes 1048576 | tf_op jit(solution)/shard_map/mul | solution.py:811

commit v6 on v5

--- a/solution.py
+++ b/solution.py
@@ -368,6 +368,7 @@
         a2a_copy(s, sector).start()
     p_all[z, core, pl.ds(pl.multiple_of(sector * 32, 32), 32), :] = parents(sector, 3)
 
+    total[...] = jnp.zeros_like(total)
 
     for copy in loads[3:]:
         copy.wait()
@@ -524,7 +525,7 @@
     mid_table(p_spread.take(2), 1 - core)
     mid_table(p_spread.take(3), 1 - core)
 
-    def middle(k):
+    def middle(k, beside=None):
         s = nth(k)
         odd = s % 2
         first = odd * 128 + (s - odd + core) * 8
@@ -536,6 +537,8 @@
                 t = t_tab[pl.ds(offset_s[first + i, j], 8), :]
                 kept = kept + p * t
             mid_sum[pl.ds(pl.multiple_of(k * 64 + i * 8, 8), 8), :] = kept
+            if beside is not None:
+                beside(i)
             return carry
 
         lax.fori_loop(0, 8, mid_box, 0)
@@ -544,22 +547,71 @@
         middle(k)
         return carry
 
+    def offset_part(plane, side, i):
+        at = plane * 2 + side
+        for part in range(t_all.shape[2] // 128):
+            row = i * (t_all.shape[2] // 8) + part * 16
+            found = t_all[plane, side, pl.ds(pl.multiple_of(row, 16), 16), :].astype(F32)
+            for half in range(2):
+                t_top[pl.ds(row * 8 + half * 64 + at, 8, stride=8), :] = found[half * 8 : half * 8 + 8]
+
+    def top_part(plane, side, i):
+        for odd in range(2):
+            found = tp_all[plane, side, pl.ds(pl.multiple_of(i * 32 + odd * 16, 16), 16), :].astype(F32)
+            first = ((2 * plane + odd) * 16 + (i * 2 + side)) * 16
+            p_top[pl.ds(pl.multiple_of(first, 16), 16), :] = found
+
     ahead = 8
-    lax.fori_loop(0, 4, middle_early, 0)
+    z_left, z_right, z_far = t_spread.left, t_spread.right, t_spread.far
+    away = 1 - core
+    lax.fori_loop(0, 2, middle_early, 0)
     tp_spread.forward()
     t_spread.forward()
     tp_spread.forward_rest()
     t_spread.forward_rest()
-    lax.fori_loop(4, ahead, middle_early, 0)
+
+    def tables2(i):
+        offset_part(z, core, i)
+        offset_part(z_left, core, i)
+        top_part(z_left, core, i)
+
+    middle(2, tables2)
+    t_spread.take(0)
+    tp_spread.take(0)
+
+    def tables3(i):
+        offset_part(z_right, core, i)
+        offset_part(z, away, i)
+        top_part(z_right, core, i)
+        top_part(z, away, i)
+
+    middle(3, tables3)
+    t_spread.take(1)
+    t_spread.take(2)
+    tp_spread.take(1)
+    tp_spread.take(2)
+
+    def tables4(i):
+        offset_part(z_left, away, i)
+        offset_part(z_right, away, i)
+        top_part(z_left, away, i)
+        top_part(z_right, away, i)
+
+    middle(4, tables4)
+    middle(5)
     tp_spread.forward_far()
     t_spread.forward_far()
-    for plane in (z, t_spread.left, t_spread.right, t_spread.far):
-        offset_table(plane, core)
-    for plane in (tp_spread.left, tp_spread.right, tp_spread.far):
-        top_table(plane, core)
-    for which in range(4):
-        offset_table(t_spread.take(which), 1 - core)
-        top_table(tp_spread.take(which), 1 - core)
+
+    def tables6(i):
+        offset_part(z_far, core, i)
+        top_part(z_far, core, i)
+
+    middle(6, tables6)
+    middle(7)
+    t_spread.take(3)
+    tp_spread.take(3)
+    offset_table(z_far, away)
+    top_table(z_far, away)
 
     behind = (trans_top_ref.shape[0] // 2) * 8
 
@@ -646,26 +698,28 @@
             children[pair * 16 : pair * 16 + 16, target] = jnp.concatenate(reals, axis=0).astype(BF16)
             children[64 + pair * 16 : 80 + pair * 16, target] = jnp.concatenate(imags, axis=0).astype(BF16)
 
-    def finish(piece_at, first, count):
+    def take_piece(piece_at, count):
         at = apart(group, piece_at)
         for slot in range(count):
-            back_copy(at * 4 + apart(inside, slot), at * 4 + apart(inside, slot)).wait_recv()
+            s = at * 4 + apart(inside, slot)
+            back_copy(s, s).wait_recv()
         for slot in range(4):
             make_children(at * 4 + slot, slot)
+
+    block = 512
+
+    def product(at, k):
         columns = pl.ds(pl.multiple_of(at * 1024, 1024), 1024)
-
-        def quarter(k, carry):
-            rows_at = pl.ds(pl.multiple_of(k * 256, 256), 256)
-            part = lax.dot_general(
-                weights[rows_at, columns], children[...], (((1,), (1,)), ((), ())), preferred_element_type=F32
-            )
-            if first:
-                total[rows_at, :] = part
-            else:
-                total[rows_at, :] += part
-            return carry
-
-        lax.fori_loop(0, 4, quarter, 0)
+        rows_at = pl.ds(k * block, block)
+        return lax.dot_general(
+            weights[rows_at, columns], children[...], (((1,), (1,)), ((), ())), preferred_element_type=F32
+        )
+
+    def finish_piece(piece_at, carry):
+        take_piece(piece_at, 4)
+        for k in range(total.shape[0] // block):
+            total[k * block : k * block + block, :] += product(apart(group, piece_at), k)
+        return carry
 
     def send_back(k, carry):
         s = nth(k)
@@ -681,16 +735,16 @@
     lax.fori_loop(ahead, SECTORS - 1, middle_and_send, 0)
     middle(SECTORS - 1)
     received[sector] = combine(SECTORS - 1)
-    finish(0, True, 4)
-    finish(1, False, 4)
-    finish(2, False, 4)
-    finish(3, False, 3)
+    lax.fori_loop(0, 3, finish_piece, 0)
+    take_piece(3, 3)
     half_rows = out_ref.shape[1]
-    for k in range(total.shape[0] // LANES):
-        columns = slice(k * LANES, k * LANES + LANES)
-        turned = jnp.transpose(total[columns, :])
-        for part in range(2):
-            out_ref[part, :, columns] = turned[part * half_rows : part * half_rows + half_rows]
+    for k in range(total.shape[0] // block):
+        part = product(group, k)
+        for n in range(k * block // 256, (k + 1) * block // 256):
+            rows_at = slice(n * 256, n * 256 + 256)
+            turned = jnp.transpose(total[rows_at, :] + part[n * 256 - k * block : n * 256 - k * block + 256])
+            for which in range(2):
+                out_ref[which, :, rows_at] = turned[which * half_rows : which * half_rows + half_rows]
 
     def wait_sent(k, carry):
         s = other(k)

time: 50 us -> 46.5 us (0.930)
  Pallas kernels: 49.1 us -> 45.5 us
    pallas_call x1, Pallas kernels: 49.1 us -> 45.5 us  [on_device(): pl.pallas_call(kernel, out_shape=VMEM(leaf_out.shape, F32), in_specs=[pl....]
where the time goes in v6:
time: 46.5 us; the launch traced here: 46.4 us
  Pallas kernels  45.5 us (98%)
  other arithmetic  0.84 us (2%)
    pallas_call x1, Pallas kernels, on_device(): pl.pallas_call(kernel, out_shape=VMEM(leaf_out.shape, F32), in_specs=[pl....  45.5 us

profile of v6, /device:TPU:1, one launch (start us, length us, event | category | flops | bytes accessed | tf_op | source)
XLA Modules:
  0.0 46.4 jit_solution(16811533935005347412)
XLA Ops:
  0.0 45.5 %far_field.1 = f32[2,64,1024]{2,1,0:T(8,128)S(1)} custom-call(bf16[2,64,1024]{2,1,0:T(8,128)(2,1)} %leaf_ref.1, bf16[1024,4096]{1,0:T(8,128)(2,1)} %matrix_ref.1, f32[8,4096]{1,0:T(8,128)} %shift_mid_ref.1, f32[632,128]{1,0:T(8,128)} %bitcast.14, f32[1264,128]{1,0:T(8,128)} %bitcast.12, bf16[256,1024]{1,0:T(8,128)(2,1)} %bitcast.13, f32[64,128]{1,0:T(8,128)} %bitcast.17, ...), custom_call_target="tpu_custom_call" | custom-call | tf_op jit(solution)/shard_map/far_field/pallas_call | solution.py:796
  45.5 0.8 %broadcast_multiply_fusion = f32[2,64,1024]{2,1,0:T(8,128)} fusion(f32[2,64,1024]{2,1,0:T(8,128)S(1)} %far_field.1), kind=kLoop, calls=%fused_computation | loop fusion | flops 131072 | bytes 1048576 | tf_op jit(solution)/shard_map/mul | solution.py:865

commit v7 on v6

--- a/solution.py
+++ b/solution.py
@@ -139,8 +139,7 @@
     lists_top,
     scaled_mid,
     scaled_top,
-    list_s,
-    offset_s,
+    near,
     list_ts,
     offset_ts,
     p_all,
@@ -172,6 +171,7 @@
     weight_sem,
     load_sem,
     index_sem,
+    near_sem,
     a2a_send,
     a2a_recv,
     swap_sem,
@@ -373,19 +373,26 @@
     for copy in loads[3:]:
         copy.wait()
     scaled = jnp.transpose(jnp.concatenate([lists_mid[0], lists_mid[1]], axis=0) * 8)
-    scaled_mid[0] = scaled[:, :entries]
-    scaled_mid[1] = scaled[:, entries:]
+    for quad_at in range(64):
+        scaled_mid[quad_at] = scaled[quad_at * 4 : quad_at * 4 + 4]
     scaled = jnp.transpose(jnp.concatenate([lists_top[0] * 16, lists_top[1] * 8], axis=0))
     scaled_top[0] = scaled[:, :entries]
     scaled_top[1] = scaled[:, entries:]
     to_smem = [
-        pltpu.make_async_copy(scaled_mid.at[0], list_s, index_sem.at[0]),
-        pltpu.make_async_copy(scaled_mid.at[1], offset_s, index_sem.at[1]),
-        pltpu.make_async_copy(scaled_top.at[0], list_ts, index_sem.at[2]),
-        pltpu.make_async_copy(scaled_top.at[1], offset_ts, index_sem.at[3]),
+        pltpu.make_async_copy(scaled_top.at[0], list_ts, index_sem.at[0]),
+        pltpu.make_async_copy(scaled_top.at[1], offset_ts, index_sem.at[1]),
     ]
     for copy in to_smem:
         copy.start()
+
+    def fetch(k, slot):
+        s = nth(k)
+        odd = s % 2
+        quad_at = odd * 32 + (s - odd + core) * 2 + slot % 2
+        return pltpu.make_async_copy(scaled_mid.at[quad_at], near.at[slot], near_sem.at[slot])
+
+    for slot in range(4):
+        fetch(slot // 2, slot).start()
 
     @pl.when(own)
     def _():
@@ -489,20 +496,6 @@
 
         lax.fori_loop(0, SECTORS // 4, four, 0)
 
-    def offset_table(plane, side):
-        at = plane * 2 + side
-
-        def four(k, carry):
-            for part in range(4):
-                found = t_all[plane, side, pl.ds(pl.multiple_of(k * 64 + part * 16, 16), 16), :].astype(F32)
-                for half in range(2):
-                    t_top[pl.ds(k * 512 + part * 128 + half * 64 + at, 8, stride=8), :] = found[
-                        half * 8 : half * 8 + 8
-                    ]
-            return carry
-
-        lax.fori_loop(0, t_all.shape[2] // 64, four, 0)
-
     mid_table(z, core)
     top_table(z, core)
     p_spread.forward()
@@ -525,46 +518,42 @@
     mid_table(p_spread.take(2), 1 - core)
     mid_table(p_spread.take(3), 1 - core)
 
-    def middle(k, beside=None):
-        s = nth(k)
-        odd = s % 2
-        first = odd * 128 + (s - odd + core) * 8
-
-        def mid_box(i, carry):
-            kept = jnp.zeros((8, LANES), F32)
-            for j in range(entries):
-                p = p_tab[pl.ds(list_s[first + i, j], 8), :]
-                t = t_tab[pl.ds(offset_s[first + i, j], 8), :]
-                kept = kept + p * t
-            mid_sum[pl.ds(pl.multiple_of(k * 64 + i * 8, 8), 8), :] = kept
-            if beside is not None:
-                beside(i)
-            return carry
-
-        lax.fori_loop(0, 8, mid_box, 0)
-
-    def middle_early(k, carry):
-        middle(k)
-        return carry
+    def middle(k, parity, more=True, beside=None):
+        for half in range(2):
+            slot = parity * 2 + half
+            fetch(k, slot).wait()
+            for i in range(4):
+                box = half * 4 + i
+                kept = jnp.zeros((8, LANES), F32)
+                for j in range(entries):
+                    p = p_tab[pl.ds(near[slot, i, j], 8), :]
+                    t = t_tab[pl.ds(near[slot, i, entries + j], 8), :]
+                    kept = kept + p * t
+                mid_sum[pl.ds(pl.multiple_of(k * 64 + box * 8, 8), 8), :] = kept
+                if beside is not None:
+                    beside(box)
+            if more:
+                fetch(k + 2, slot).start()
 
     def offset_part(plane, side, i):
         at = plane * 2 + side
         for part in range(t_all.shape[2] // 128):
             row = i * (t_all.shape[2] // 8) + part * 16
-            found = t_all[plane, side, pl.ds(pl.multiple_of(row, 16), 16), :].astype(F32)
+            found = t_all[plane, side, row : row + 16, :].astype(F32)
             for half in range(2):
                 t_top[pl.ds(row * 8 + half * 64 + at, 8, stride=8), :] = found[half * 8 : half * 8 + 8]
 
     def top_part(plane, side, i):
         for odd in range(2):
-            found = tp_all[plane, side, pl.ds(pl.multiple_of(i * 32 + odd * 16, 16), 16), :].astype(F32)
+            found = tp_all[plane, side, i * 32 + odd * 16 : i * 32 + odd * 16 + 16, :].astype(F32)
             first = ((2 * plane + odd) * 16 + (i * 2 + side)) * 16
             p_top[pl.ds(pl.multiple_of(first, 16), 16), :] = found
 
-    ahead = 8
+    ahead = 10
     z_left, z_right, z_far = t_spread.left, t_spread.right, t_spread.far
     away = 1 - core
-    lax.fori_loop(0, 2, middle_early, 0)
+    middle(0, 0)
+    middle(1, 1)
     tp_spread.forward()
     t_spread.forward()
     tp_spread.forward_rest()
@@ -575,7 +564,7 @@
         offset_part(z_left, core, i)
         top_part(z_left, core, i)
 
-    middle(2, tables2)
+    middle(2, 0, True, tables2)
     t_spread.take(0)
     tp_spread.take(0)
 
@@ -585,7 +574,7 @@
         top_part(z_right, core, i)
         top_part(z, away, i)
 
-    middle(3, tables3)
+    middle(3, 1, True, tables3)
     t_spread.take(1)
     t_spread.take(2)
     tp_spread.take(1)
@@ -597,21 +586,26 @@
         top_part(z_left, away, i)
         top_part(z_right, away, i)
 
-    middle(4, tables4)
-    middle(5)
+    middle(4, 0, True, tables4)
+    middle(5, 1)
+    middle(6, 0)
     tp_spread.forward_far()
     t_spread.forward_far()
 
-    def tables6(i):
+    def tables7(i):
         offset_part(z_far, core, i)
         top_part(z_far, core, i)
 
-    middle(6, tables6)
-    middle(7)
+    middle(7, 1, True, tables7)
+    middle(8, 0)
     t_spread.take(3)
     tp_spread.take(3)
-    offset_table(z_far, away)
-    top_table(z_far, away)
+
+    def tables9(i):
+        offset_part(z_far, away, i)
+        top_part(z_far, away, i)
+
+    middle(9, 1, True, tables9)
 
     behind = (trans_top_ref.shape[0] // 2) * 8
 
@@ -727,13 +721,17 @@
         back_copy(s, sector).start()
         return carry
 
-    def middle_and_send(k, carry):
-        middle(k)
-        return send_back(k, carry)
+    def pair_and_send(pair_at, carry):
+        for parity in range(2):
+            middle(pair_at * 2 + parity, parity)
+            send_back(pair_at * 2 + parity, carry)
+        return carry
 
     lax.fori_loop(0, ahead, send_back, 0)
-    lax.fori_loop(ahead, SECTORS - 1, middle_and_send, 0)
-    middle(SECTORS - 1)
+    lax.fori_loop(ahead // 2, SECTORS // 2 - 1, pair_and_send, 0)
+    middle(SECTORS - 2, 0, False)
+    send_back(SECTORS - 2, 0)
+    middle(SECTORS - 1, 1, False)
     received[sector] = combine(SECTORS - 1)
     lax.fori_loop(0, 3, finish_piece, 0)
     take_piece(3, 3)
@@ -808,10 +806,9 @@
             VMEM((64, LANES), F32),
             VMEM((2, entries, 256), jnp.int32),
             VMEM((2, entries, 128), jnp.int32),
-            VMEM((2, 256, entries), jnp.int32),
+            VMEM((64, 4, 2 * entries), jnp.int32),
             VMEM((2, 128, entries), jnp.int32),
-            pltpu.SMEM((256, entries), jnp.int32),
-            pltpu.SMEM((256, entries), jnp.int32),
+            pltpu.SMEM((4, 4, 2 * entries), jnp.int32),
             pltpu.SMEM((128, entries), jnp.int32),
             pltpu.SMEM((128, entries), jnp.int32),
             VMEM((PLANES, 2, 512, LANES), BF16),
@@ -842,6 +839,7 @@
             VMEM((interp_mid.shape[0], rows), F32),
             DMA((4,)),
             DMA((7,)),
+            DMA((2,)),
             DMA((4,)),
             DMA((SECTORS,)),
             DMA((SECTORS,)),

time: 46.5 us -> 44.6 us (0.959)
  Pallas kernels: 45.5 us -> 43.6 us
    pallas_call x1, Pallas kernels: 45.5 us -> 43.6 us  [on_device(): pl.pallas_call(kernel, out_shape=VMEM(leaf_out.shape, F32), in_specs=[pl....]
where the time goes in v7:
time: 44.6 us; the launch traced here: 44.5 us
  Pallas kernels  43.6 us (98%)
  other arithmetic  0.84 us (2%)
    pallas_call x1, Pallas kernels, on_device(): pl.pallas_call(kernel, out_shape=VMEM(leaf_out.shape, F32), in_specs=[pl....  43.6 us

profile of v7, /device:TPU:1, one launch (start us, length us, event | category | flops | bytes accessed | tf_op | source)
XLA Modules:
  0.0 44.5 jit_solution(2467643142887806823)
XLA Ops:
  0.0 43.6 %far_field.1 = f32[2,64,1024]{2,1,0:T(8,128)S(1)} custom-call(bf16[2,64,1024]{2,1,0:T(8,128)(2,1)} %leaf_ref.1, bf16[1024,4096]{1,0:T(8,128)(2,1)} %matrix_ref.1, f32[8,4096]{1,0:T(8,128)} %shift_mid_ref.1, f32[632,128]{1,0:T(8,128)} %bitcast.14, f32[1264,128]{1,0:T(8,128)} %bitcast.12, bf16[256,1024]{1,0:T(8,128)(2,1)} %bitcast.13, f32[64,128]{1,0:T(8,128)} %bitcast.17, ...), custom_call_target="tpu_custom_call" | custom-call | tf_op jit(solution)/shard_map/far_field/pallas_call | solution.py:794
  43.7 0.8 %broadcast_multiply_fusion = f32[2,64,1024]{2,1,0:T(8,128)} fusion(f32[2,64,1024]{2,1,0:T(8,128)S(1)} %far_field.1), kind=kLoop, calls=%fused_computation | loop fusion | flops 131072 | bytes 1048576 | tf_op jit(solution)/shard_map/mul | solution.py:863

commit v8 on v7

--- a/solution.py
+++ b/solution.py
@@ -140,8 +140,8 @@
     scaled_mid,
     scaled_top,
     near,
-    list_ts,
-    offset_ts,
+    own_top,
+    near_top,
     p_all,
     tp_all,
     t_all,
@@ -246,16 +246,24 @@
     for copy in loads[:3]:
         copy.start()
 
-    def weight_copy(piece_at):
+    def weight_copies(piece_at):
         columns = pl.ds(pl.multiple_of(apart(group, piece_at) * 1024, 1024), 1024)
-        return pltpu.make_async_copy(matrix_ref.at[:, columns], weights.at[:, columns], weight_sem.at[piece_at])
-
-    for piece_at in range(4):
-        weight_copy(piece_at).start()
-    for copy in loads[3:]:
+        size = matrix_ref.shape[0] // 4
+        return [
+            pltpu.make_async_copy(
+                matrix_ref.at[part * size : part * size + size, columns],
+                weights.at[part * size : part * size + size, columns],
+                weight_sem.at[piece_at * 4 + part],
+            )
+            for part in range(4)
+        ]
+
+    for copy in weight_copies(0):
         copy.start()
 
     loads[0].wait()
+    for copy in weight_copies(1):
+        copy.start()
     rows = 2 * leaf.shape[1]
     target = lax.broadcasted_iota(jnp.int32, (rows, rows), 0)
     source = lax.broadcasted_iota(jnp.int32, (rows, rows), 1)
@@ -265,6 +273,11 @@
     leaf_rows[...] = jnp.dot(order, both, preferred_element_type=F32).astype(BF16)
 
     loads[1].wait()
+    for piece_at in (2, 3):
+        for copy in weight_copies(piece_at):
+            copy.start()
+    for copy in loads[3:]:
+        copy.start()
     used = trans_top.shape[0]
     piece[0:used, :] = trans_top[...].astype(BF16)
     piece[used:, :] = jnp.zeros((piece.shape[0] - used, LANES), BF16)
@@ -329,7 +342,8 @@
         )
 
     def make_four(piece_at):
-        weight_copy(piece_at).wait()
+        for copy in weight_copies(piece_at):
+            copy.wait()
         for slot in range(4):
             s = nth(piece_at * 4 + slot)
             sending[s] = parents(s, slot)
@@ -361,12 +375,14 @@
         return carry
 
     lax.fori_loop(1, 3, send_four, 0)
-    weight_copy(3).wait()
+    for copy in weight_copies(3):
+        copy.wait()
     for slot in range(3):
         s = nth(12 + slot)
         sending[s] = parents(s, slot)
-        a2a_copy(s, sector).start()
     p_all[z, core, pl.ds(pl.multiple_of(sector * 32, 32), 32), :] = parents(sector, 3)
+    for slot in range(3):
+        a2a_copy(nth(12 + slot), sector).start()
 
     total[...] = jnp.zeros_like(total)
 
@@ -376,12 +392,9 @@
     for quad_at in range(64):
         scaled_mid[quad_at] = scaled[quad_at * 4 : quad_at * 4 + 4]
     scaled = jnp.transpose(jnp.concatenate([lists_top[0] * 16, lists_top[1] * 8], axis=0))
-    scaled_top[0] = scaled[:, :entries]
-    scaled_top[1] = scaled[:, entries:]
-    to_smem = [
-        pltpu.make_async_copy(scaled_top.at[0], list_ts, index_sem.at[0]),
-        pltpu.make_async_copy(scaled_top.at[1], offset_ts, index_sem.at[1]),
-    ]
+    scaled_top[...] = scaled
+    own_top[...] = scaled_top[pl.ds(z * 32 + core, 16, stride=2), :]
+    to_smem = [pltpu.make_async_copy(own_top, near_top, index_sem.at[0])]
     for copy in to_smem:
         copy.start()
 
@@ -500,12 +513,13 @@
     top_table(z, core)
     p_spread.forward()
     tp_spread.start_own()
-    p_spread.forward_rest()
 
     @pl.when(jnp.logical_not(own))
     def _():
         swap_copy.wait()
         t_spread.start_own()
+
+    p_spread.forward_rest()
 
     mid_table(p_spread.left, core)
     mid_table(p_spread.right, core)
@@ -609,13 +623,12 @@
 
     behind = (trans_top_ref.shape[0] // 2) * 8
 
-    def top_box(k, carry):
-        odd = k % 2
-        column = (2 * z + odd) * 16 + (k - odd + core)
+    def top_box(k):
+        row = (k % 2) * 8 + k // 2
         sums = [jnp.zeros((8, LANES), F32) for _ in range(4)]
         for j in range(entries):
-            n = list_ts[column, j]
-            o = offset_ts[column, j]
+            n = near_top[row, j]
+            o = near_top[row, entries + j]
             pr = p_top[pl.ds(n, 8), :]
             pi = p_top[pl.ds(n + 8, 8), :]
             tr = t_top[pl.ds(o, 8), :]
@@ -623,11 +636,11 @@
             sums = [sums[0] + pr * tr, sums[1] + pi * ti, sums[2] + pr * ti, sums[3] + pi * tr]
         real = (sums[0] - sums[1]).astype(BF16).astype(F32)
         imag = (sums[2] + sums[3]).astype(BF16).astype(F32)
-        top_sum[pl.ds(pl.multiple_of(k * 16, 16), 8), :] = real
-        top_sum[pl.ds(pl.multiple_of(k * 16 + 8, 8), 8), :] = imag
-        return carry
-
-    lax.fori_loop(0, SECTORS, top_box, 0)
+        top_sum[k * 16 : k * 16 + 8, :] = real
+        top_sum[k * 16 + 8 : k * 16 + 16, :] = imag
+
+    for k in range(SECTORS):
+        top_box(k)
 
     def top_children(part, carry):
         lanes = pl.ds(pl.multiple_of(part * LANES, LANES), LANES)
@@ -807,10 +820,10 @@
             VMEM((2, entries, 256), jnp.int32),
             VMEM((2, entries, 128), jnp.int32),
             VMEM((64, 4, 2 * entries), jnp.int32),
-            VMEM((2, 128, entries), jnp.int32),
+            VMEM((128, 2 * entries), jnp.int32),
             pltpu.SMEM((4, 4, 2 * entries), jnp.int32),
-            pltpu.SMEM((128, entries), jnp.int32),
-            pltpu.SMEM((128, entries), jnp.int32),
+            VMEM((16, 2 * entries), jnp.int32),
+            pltpu.SMEM((16, 2 * entries), jnp.int32),
             VMEM((PLANES, 2, 512, LANES), BF16),
             VMEM((PLANES, 2, 256, LANES), BF16),
             VMEM((PLANES, 2, padded, LANES), BF16),
@@ -837,7 +850,7 @@
             VMEM((SECTORS, 16, 256), BF16),
             VMEM((rows, 1024), BF16),
             VMEM((interp_mid.shape[0], rows), F32),
-            DMA((4,)),
+            DMA((16,)),
             DMA((7,)),
             DMA((2,)),
             DMA((4,)),

time: 44.6 us -> 43.9 us (0.984)
  Pallas kernels: 43.6 us -> 42.9 us
    pallas_call x1, Pallas kernels: 43.6 us -> 42.9 us  [on_device(): pl.pallas_call(kernel, out_shape=VMEM(leaf_out.shape, F32), in_specs=[pl....]
where the time goes in v8:
time: 43.9 us; the launch traced here: 43.8 us
  Pallas kernels  42.9 us (98%)
  other arithmetic  0.84 us (2%)
    pallas_call x1, Pallas kernels, on_device(): pl.pallas_call(kernel, out_shape=VMEM(leaf_out.shape, F32), in_specs=[pl....  42.9 us

profile of v8, /device:TPU:1, one launch (start us, length us, event | category | flops | bytes accessed | tf_op | source)
XLA Modules:
  0.0 43.8 jit_solution(17968194151859720289)
XLA Ops:
  0.0 42.9 %far_field.1 = f32[2,64,1024]{2,1,0:T(8,128)S(1)} custom-call(bf16[2,64,1024]{2,1,0:T(8,128)(2,1)} %leaf_ref.1, bf16[1024,4096]{1,0:T(8,128)(2,1)} %matrix_ref.1, f32[8,4096]{1,0:T(8,128)} %shift_mid_ref.1, f32[632,128]{1,0:T(8,128)} %bitcast.14, f32[1264,128]{1,0:T(8,128)} %bitcast.12, bf16[256,1024]{1,0:T(8,128)(2,1)} %bitcast.13, f32[64,128]{1,0:T(8,128)} %bitcast.17, ...), custom_call_target="tpu_custom_call" | custom-call | tf_op jit(solution)/shard_map/far_field/pallas_call | solution.py:807
  42.9 0.8 %broadcast_multiply_fusion = f32[2,64,1024]{2,1,0:T(8,128)} fusion(f32[2,64,1024]{2,1,0:T(8,128)S(1)} %far_field.1), kind=kLoop, calls=%fused_computation | loop fusion | flops 131072 | bytes 1048576 | tf_op jit(solution)/shard_map/mul | solution.py:876

commit v9 on v8

--- a/solution.py
+++ b/solution.py
@@ -567,11 +567,12 @@
     z_left, z_right, z_far = t_spread.left, t_spread.right, t_spread.far
     away = 1 - core
     middle(0, 0)
-    middle(1, 1)
     tp_spread.forward()
     t_spread.forward()
     tp_spread.forward_rest()
     t_spread.forward_rest()
+
+    middle(1, 1)
 
     def tables2(i):
         offset_part(z, core, i)

time: 43.9 us -> 43.3 us (0.986)
  Pallas kernels: 42.9 us -> 42.4 us
    pallas_call x1, Pallas kernels: 42.9 us -> 42.4 us  [on_device(): pl.pallas_call(kernel, out_shape=VMEM(leaf_out.shape, F32), in_specs=[pl....]
where the time goes in v9:
time: 43.3 us; the launch traced here: 43.2 us
  Pallas kernels  42.4 us (98%)
  other arithmetic  0.84 us (2%)
    pallas_call x1, Pallas kernels, on_device(): pl.pallas_call(kernel, out_shape=VMEM(leaf_out.shape, F32), in_specs=[pl....  42.4 us

profile of v9, /device:TPU:1, one launch (start us, length us, event | category | flops | bytes accessed | tf_op | source)
XLA Modules:
  0.0 43.2 jit_solution(9904360789809017065)
XLA Ops:
  0.0 42.4 %far_field.1 = f32[2,64,1024]{2,1,0:T(8,128)S(1)} custom-call(bf16[2,64,1024]{2,1,0:T(8,128)(2,1)} %leaf_ref.1, bf16[1024,4096]{1,0:T(8,128)(2,1)} %matrix_ref.1, f32[8,4096]{1,0:T(8,128)} %shift_mid_ref.1, f32[632,128]{1,0:T(8,128)} %bitcast.14, f32[1264,128]{1,0:T(8,128)} %bitcast.12, bf16[256,1024]{1,0:T(8,128)(2,1)} %bitcast.13, f32[64,128]{1,0:T(8,128)} %bitcast.17, ...), custom_call_target="tpu_custom_call" | custom-call | tf_op jit(solution)/shard_map/far_field/pallas_call | solution.py:808
  42.4 0.8 %broadcast_multiply_fusion = f32[2,64,1024]{2,1,0:T(8,128)} fusion(f32[2,64,1024]{2,1,0:T(8,128)S(1)} %far_field.1), kind=kLoop, calls=%fused_computation | loop fusion | flops 131072 | bytes 1048576 | tf_op jit(solution)/shard_map/mul | solution.py:877
